TPU v7x, 32 devices: a 4x2x2 block of a 4x4x8 slice. The times are simulated.
32 devices in a mesh: data: 4 (over y, z), tensor: 8 (over x, core).
Axes of the slice: x: 4, y: 2, z: 2, core: 2. Of those that a mesh axis runs over, the one named last changes fastest.
The devices are a block of a 4x4x8 slice.
Arguments:
- x_in: bfloat16 [64, 128, 3072], P('data'), parts along dimension 0
- adapter_ids: int32 [64], P('data'), parts along dimension 0
- gain_attn: float32 [3072], replicated
- gain_mlp: float32 [3072], replicated
- w_q: bfloat16 [3072, 16, 256], P(None, 'tensor')
- w_k: bfloat16 [3072, 16, 256], P(None, 'tensor')
- w_v: bfloat16 [3072, 16, 256], P(None, 'tensor')
- w_o: bfloat16 [16, 256, 3072], P('tensor')
- w_gate: bfloat16 [3072, 24576], P(None, 'tensor')
- w_up: bfloat16 [3072, 24576], P(None, 'tensor')
- w_down: bfloat16 [24576, 3072], P('tensor')
- a_q: bfloat16 [8, 3072, 256], P(None, None, 'tensor')
- b_q: bfloat16 [8, 256, 16, 256], P(None, None, 'tensor')
- a_k: bfloat16 [8, 3072, 256], P(None, None, 'tensor')
- b_k: bfloat16 [8, 256, 16, 256], P(None, None, 'tensor')
- a_v: bfloat16 [8, 3072, 256], P(None, None, 'tensor')
- b_v: bfloat16 [8, 256, 16, 256], P(None, None, 'tensor')
- a_o: bfloat16 [8, 16, 256, 256], P(None, 'tensor')
- b_o: bfloat16 [8, 256, 3072], P(None, None, 'tensor')
- a_gate: bfloat16 [8, 3072, 256], P(None, None, 'tensor')
- b_gate: bfloat16 [8, 256, 24576], P(None, None, 'tensor')
- a_up: bfloat16 [8, 3072, 256], P(None, None, 'tensor')
- b_up: bfloat16 [8, 256, 24576], P(None, None, 'tensor')
- a_down: bfloat16 [8, 24576, 256], P(None, 'tensor')
- b_down: bfloat16 [8, 256, 3072], P(None, None, 'tensor')
Outputs:
- output: bfloat16 [64, 128, 3072], P('data'), parts along dimension 0
There are 4 independent parts. A program takes and returns all parts, laid end to end along the dimension named above; an argument that names none is the same for every part.
All inputs are finite; a program needn't handle non-finite values.
Results may differ from a plain program's by a relative error of at most 0.02.
Values are sent between devices in bfloat16 or wider.
A program may use at most 768 MiB of HBM per device.

v0:
```python
import jax
import jax.numpy as jnp
from jax import lax
from jax.sharding import PartitionSpec as P

ALPHA = 16.0
ROPE_BASE = 10000.0
EPSILON = 1e-5


def rms_gain(act_in, gain_vec):
    act_f32 = act_in.astype(jnp.float32)
    inv_rms = lax.rsqrt(jnp.mean(act_f32 * act_f32, axis=-1, keepdims=True) + EPSILON)
    return (act_f32 * inv_rms * gain_vec).astype(jnp.bfloat16)


def rope_rotate(head_vals):
    seq_len = head_vals.shape[1]
    head_dim = head_vals.shape[-1]
    half_dim = head_dim // 2
    inv_freq = ROPE_BASE ** (-2.0 * jnp.arange(half_dim, dtype=jnp.float32) / head_dim)
    angle_tab = jnp.arange(seq_len, dtype=jnp.float32)[:, None] * inv_freq[None, :]
    cos_tab = jnp.cos(angle_tab)[:, None, :]
    sin_tab = jnp.sin(angle_tab)[:, None, :]
    first_half = head_vals[..., :half_dim]
    second_half = head_vals[..., half_dim:]
    return jnp.concatenate([first_half * cos_tab - second_half * sin_tab, second_half * cos_tab + first_half * sin_tab], axis=-1)


def causal_attention(q_heads, k_heads, v_heads):
    batch_size, seq_len, q_count, head_dim = q_heads.shape
    kv_count = k_heads.shape[2]
    q_group = q_heads.reshape(batch_size, seq_len, kv_count, q_count // kv_count, head_dim)
    scores = jnp.einsum('bskgd,btkd->bkgst', q_group, k_heads, preferred_element_type=jnp.float32) * head_dim ** -0.5
    causal = jnp.arange(seq_len)[:, None] >= jnp.arange(seq_len)[None, :]
    attn_prob = jax.nn.softmax(jnp.where(causal, scores, -1e30), axis=-1).astype(jnp.bfloat16)
    mixed_out = jnp.einsum('bkgst,btkd->bskgd', attn_prob, v_heads, preferred_element_type=jnp.float32)
    return mixed_out.astype(jnp.bfloat16).reshape(batch_size, seq_len, q_count, head_dim)


def solution(mesh):
    tp_size = mesh.shape['tensor']
    head_split = P(None, 'tensor', None)
    last_split = P(None, None, 'tensor')
    b_head_split = P(None, None, 'tensor', None)
    in_specs = (P('data', None, None), P('data'), P(None), P(None),
                head_split, head_split, head_split, P('tensor', None, None),
                P(None, 'tensor'), P(None, 'tensor'), P('tensor', None),
                last_split, b_head_split, last_split, b_head_split, last_split, b_head_split,
                P(None, 'tensor', None, None), last_split,
                last_split, last_split, last_split, last_split,
                P(None, 'tensor', None), last_split)

    def local_layer(x_in, adapter_ids, gain_attn, gain_mlp, w_q, w_k, w_v, w_o, w_gate, w_up, w_down, a_q, b_q, a_k, b_k, a_v, b_v, a_o, b_o, a_gate, b_gate, a_up, b_up, a_down, b_down):
        value_a10 = ALPHA / b_q.shape[1]
        shard_width = x_in.shape[2] // tp_size
        my_index = lax.axis_index('tensor')

        def per_sequence(table_stack):
            return jnp.take(table_stack, adapter_ids, axis=0)

        def column_proj(act_in, weight, a_stack, b_stack, base_form, up_form):
            low_part = jnp.einsum('bsd,bdr->bsr', act_in, per_sequence(a_stack), preferred_element_type=jnp.float32)
            low_rank = lax.all_gather(low_part.astype(jnp.bfloat16), 'tensor', axis=2, tiled=True)
            base_out = jnp.einsum(base_form, act_in, weight, preferred_element_type=jnp.float32)
            return base_out + value_a10 * jnp.einsum(up_form, low_rank, per_sequence(b_stack), preferred_element_type=jnp.float32)

        def row_proj(act_in, weight, a_stack, b_stack, base_form, low_form, resid_shard):
            base_part = jnp.einsum(base_form, act_in, weight, preferred_element_type=jnp.float32).astype(jnp.bfloat16)
            low_part = jnp.einsum(low_form, act_in, per_sequence(a_stack), preferred_element_type=jnp.float32).astype(jnp.bfloat16)
            low_rank = lax.psum(low_part, 'tensor')
            base_shard = lax.psum_scatter(base_part, 'tensor', scatter_dimension=2, tiled=True)
            delta_out = jnp.einsum('bsr,brd->bsd', low_rank, per_sequence(b_stack), preferred_element_type=jnp.float32)
            out_shard = (resid_shard.astype(jnp.float32) + base_shard.astype(jnp.float32) + value_a10 * delta_out).astype(jnp.bfloat16)
            return out_shard, lax.all_gather(out_shard, 'tensor', axis=2, tiled=True)

        h_attn = rms_gain(x_in, gain_attn)
        z_q = column_proj(h_attn, w_q, a_q, b_q, 'bsd,dhe->bshe', 'bsr,brhe->bshe')
        z_k = column_proj(h_attn, w_k, a_k, b_k, 'bsd,dhe->bshe', 'bsr,brhe->bshe')
        z_v = column_proj(h_attn, w_v, a_v, b_v, 'bsd,dhe->bshe', 'bsr,brhe->bshe')
        attn_out = causal_attention(rope_rotate(z_q).astype(jnp.bfloat16), rope_rotate(z_k).astype(jnp.bfloat16), z_v.astype(jnp.bfloat16))
        x_shard = lax.dynamic_slice_in_dim(x_in, my_index * shard_width, shard_width, axis=2)
        mid_shard, x_mid = row_proj(attn_out, w_o, a_o, b_o, 'bshe,hed->bsd', 'bshe,bher->bsr', x_shard)
        h_mlp = rms_gain(x_mid, gain_mlp)
        z_gate = column_proj(h_mlp, w_gate, a_gate, b_gate, 'bsd,df->bsf', 'bsr,brf->bsf')
        z_up = column_proj(h_mlp, w_up, a_up, b_up, 'bsd,df->bsf', 'bsr,brf->bsf')
        hidden = (jax.nn.silu(z_gate) * z_up).astype(jnp.bfloat16)
        return row_proj(hidden, w_down, a_down, b_down, 'bsf,fd->bsd', 'bsf,bfr->bsr', mid_shard)[1]

    return jax.shard_map(local_layer, mesh=mesh, in_specs=in_specs, out_specs=P('data', None, None), check_vma=False)
```

profile of v0, /device:TPU:81, one launch (start us, length us, event | category | flops | bytes accessed | tf_op | source)
XLA Modules:
  0.0 902.7 jit_solution(8689278094167322345)
XLA Ops:
  19.1 10.7 %fusion.116 = bf16[16,128,32]{1,2,0:T(8,128)(2,1)} fusion(bf16[16,3072,32]{1,2,0:T(8,128)(2,1)} %gather_fusion.6, pred[16]{0:T(512)(128)(4,1)S(1)} %compare_and_fusion, bf16[16,128,3072]{2,1,0:T(8,128)(2,1)} %param.33, f32[3072]{0:T(1024)S(1)} %copy-done.20, f32[16,128]{1,0:T(8,128)S(1)} %add_rsqrt_fusion.1), kind=kOutput, calls=%fused_computation.127 | convolution fusion | flops 429457408 | bytes 15880208 | tf_op jit(solution)/shard_map/bsd,bdr->bsr/dot_general | solution.py:63
  33.8 10.7 %fusion.113 = bf16[16,128,32]{1,2,0:T(8,128)(2,1)} fusion(bf16[16,3072,32]{1,2,0:T(8,128)(2,1)} %gather_fusion.4, pred[16]{0:T(512)(128)(4,1)S(1)} %compare_and_fusion, bf16[16,128,3072]{2,1,0:T(8,128)(2,1)} %param.33, f32[3072]{0:T(1024)S(1)} %copy-done.20, f32[16,128]{1,0:T(8,128)S(1)} %add_rsqrt_fusion.1), kind=kOutput, calls=%fused_computation.126 | convolution fusion | flops 429457408 | bytes 15880208 | tf_op jit(solution)/shard_map/bsd,bdr->bsr/dot_general | solution.py:63
  48.9 9.9 %fusion.66 = bf16[16,128,32]{1,2,0:T(8,128)(2,1)S(1)} fusion(bf16[16,3072,32]{1,2,0:T(8,128)(2,1)} %gather_fusion.2, pred[16]{0:T(512)(128)(4,1)S(1)} %compare_and_fusion, bf16[16,128,3072]{2,1,0:T(8,128)(2,1)} %param.33, f32[3072]{0:T(1024)S(1)} %copy-done.20, f32[16,128]{1,0:T(8,128)S(1)} %add_rsqrt_fusion.1), kind=kOutput, calls=%fused_computation.86 | convolution fusion | flops 429391872 | bytes 15880208 | tf_op jit(solution)/shard_map/bsd,bdr->bsr/dot_general | solution.py:63
  59.7 11.5 %gather_fusion.3 = bf16[16,256,2,256]{3,2,1,0:T(2,128)(2,1)} fusion(bf16[8,256,2,256]{3,2,1,0:T(2,128)(2,1)} %param.49, s32[1024]{0:T(1024)S(1)} %pad_clamp_fusion), kind=kCustom, calls=%fused_computation.1.clone | custom fusion | bytes 8388672 | tf_op jit(solution)/shard_map/jit(_take)/gather | solution.py:60
  71.2 11.5 %gather_fusion.5 = bf16[16,256,2,256]{3,2,1,0:T(2,128)(2,1)} fusion(bf16[8,256,2,256]{3,2,1,0:T(2,128)(2,1)} %param.47, s32[1024]{0:T(1024)S(1)} %pad_clamp_fusion), kind=kCustom, calls=%fused_computation.8.clone | custom fusion | bytes 8388672 | tf_op jit(solution)/shard_map/jit(_take)/gather | solution.py:60
  82.8 11.5 %gather_fusion.7 = bf16[16,256,2,256]{3,2,1,0:T(2,128)(2,1)} fusion(bf16[8,256,2,256]{3,2,1,0:T(2,128)(2,1)} %param.45, s32[1024]{0:T(1024)S(1)} %pad_clamp_fusion), kind=kCustom, calls=%fused_computation.9.clone | custom fusion | bytes 8388672 | tf_op jit(solution)/shard_map/jit(_take)/gather | solution.py:60
  94.3 12.1 %fusion.21 = f32[16,128,2,256]{3,1,2,0:T(8,128)} fusion(bf16[3072,2,256]{2,1,0:T(2,128)(2,1)} %param.37, bf16[16,128,3072]{2,1,0:T(8,128)(2,1)} %param.33, f32[3072]{0:T(1024)S(1)} %copy-done.20, f32[16,128]{1,0:T(8,128)S(1)} %add_rsqrt_fusion.1), kind=kOutput, calls=%fused_computation.43 | convolution fusion | flops 6467616768 | bytes 19943424 | tf_op jit(solution)/shard_map/bsd,dhe->bshe/dot_general | solution.py:65
  106.4 11.4 %fusion.23 = f32[16,128,2,256]{3,1,2,0:T(8,128)} fusion(bf16[3072,2,256]{2,1,0:T(2,128)(2,1)S(1)} %copy-done.18, bf16[16,128,3072]{2,1,0:T(8,128)(2,1)} %param.33, f32[3072]{0:T(1024)S(1)} %copy-done.20, f32[16,128]{1,0:T(8,128)S(1)} %add_rsqrt_fusion.1), kind=kOutput, calls=%fused_computation.45 | convolution fusion | flops 6467616768 | bytes 19943424 | tf_op jit(solution)/shard_map/bsd,dhe->bshe/dot_general | solution.py:65
  118.2 11.2 %fusion.25 = f32[16,128,2,256]{3,1,2,0:T(8,128)} fusion(bf16[3072,2,256,1]{2,1,0,3:T(2,128)(2,1)S(1)} %bitcast.109, bf16[16,128,3072]{2,1,0:T(8,128)(2,1)} %param.33, f32[3072]{0:T(1024)S(1)} %copy-done.20, f32[16,128]{1,0:T(8,128)S(1)} %add_rsqrt_fusion.1), kind=kOutput, calls=%fused_computation.47 | convolution fusion | flops 6467616768 | bytes 19943424 | tf_op jit(solution)/shard_map/bsd,dhe->bshe/dot_general | solution.py:65
  129.4 12.7 %broadcast_select_fusion = (bf16[16,256,2,256]{3,2,1,0:T(2,128)(2,1)}, bf16[16,256,2,256]{3,2,1,0:T(2,128)(2,1)}, bf16[16,256,2,256]{3,2,1,0:T(2,128)(2,1)}) fusion(bf16[16,256,2,256]{3,2,1,0:T(2,128)(2,1)S(1)} %copy-done.9, pred[16]{0:T(512)(128)(4,1)S(1)} %compare_and_fusion, bf16[16,256,2,256]{3,2,1,0:T(2,128)(2,1)S(1)} %copy-done.8, ...), kind=kLoop, calls=%fused_computation.52 | loop fusion | flops 6291456 | bytes 25165840 | tf_op jit(solution)/shard_map/jit(_take)/select_n | solution.py:60
  165.3 11.3 %bitcast_convert_fusion = bf16[16,128,3072]{2,1,0:T(8,128)(2,1)} fusion(bf16[2,256,3072]{2,1,0:T(8,128)(2,1)S(1)} %copy-done, bf16[16,2,256,128]{3,2,1,0:T(8,128)(2,1)} %convolution_convert_fusion), kind=kOutput, calls=%fused_computation.24 | convolution fusion | flops 6448742400 | bytes 17825792 | tf_op jit(solution)/shard_map/bshe,hed->bsd/dot_general | solution.py:69
  176.5 16.7 %copy.52 = bf16[16,128,3072]{1,0,2:T(8,128)(2,1)} copy(bf16[16,128,3072]{2,1,0:T(8,128)(2,1)} %bitcast_convert_fusion) | data formatting | bytes 25165824
  193.2 13.1 %copy.92 = bf16[384,8,16,128]{3,1,2,0:T(8,128)(2,1)} copy(bf16[384,8,16,128]{3,2,1,0:T(8,128)(2,1)} %bitcast.103) | data formatting | bytes 25165824
  218.4 61.2 %reduce-scatter.7.cloned.1.call-done = bf16[384,2048]{1,0:T(8,128)(2,1)} async-done(((bf16[3072,2048]{1,0:T(8,128)(2,1)}), bf16[384,2048]{1,0:T(8,128)(2,1)}) %reduce-scatter.7.cloned.1.call-update) | async-done | bytes 1572880
  282.7 53.5 %all-reduce.3.cloned.1.call-done = bf16[16,128,256]{2,1,0:T(8,128)(2,1)} async-done(((bf16[16,128,256]{2,1,0:T(8,128)(2,1)}), bf16[16,128,256]{2,1,0:T(8,128)(2,1)}) %all-reduce.3.cloned.1.call-update) | async-done | bytes 1048592 | tf_op jit(solution)/shard_map/psum | solution.py:71
  343.8 63.4 %all-gather.14.cloned.1.call-done = bf16[16,128,3072]{2,1,0:T(8,128)(2,1)} async-done(((bf16[16,128,384]{2,1,0:T(8,128)(2,1)}), bf16[16,128,3072]{2,1,0:T(8,128)(2,1)}) %all-gather.14.cloned.1.call-update) | async-done | bytes 12582928 | tf_op jit(solution)/shard_map/all_gather | solution.py:75
  424.7 14.8 %gather_fusion.10 = bf16[16,256,3072]{2,1,0:T(8,128)(2,1)} fusion(bf16[8,256,3072]{2,1,0:T(8,128)(2,1)} %param.53, s32[1024]{0:T(1024)S(1)} %pad_clamp_fusion), kind=kCustom, calls=%fused_computation.3.clone | custom fusion | bytes 50331712 | tf_op jit(solution)/shard_map/jit(_take)/gather | solution.py:60
  441.9 14.7 %gather_fusion.12 = bf16[16,256,3072]{2,1,0:T(8,128)(2,1)} fusion(bf16[8,256,3072]{2,1,0:T(8,128)(2,1)} %param.55, s32[1024]{0:T(1024)S(1)} %pad_clamp_fusion), kind=kCustom, calls=%fused_computation.11.clone | custom fusion | bytes 50331712 | tf_op jit(solution)/shard_map/jit(_take)/gather | solution.py:60
  456.6 9.8 %fusion.124 = bf16[16,128,32]{1,2,0:T(8,128)(2,1)} fusion(bf16[16,3072,32]{1,2,0:T(8,128)(2,1)S(1)} %copy-done.5, pred[16]{0:T(512)(128)(4,1)S(1)} %compare_and_fusion, bf16[16,128,3072]{2,1,0:T(8,128)(2,1)} %all-gather.14.cloned.1.call-done, f32[3072]{0:T(1024)S(1)} %copy-done.21, f32[16,128]{1,0:T(8,128)S(1)} %add_rsqrt_fusion), kind=kOutput, calls=%fused_computation.129 | convolution fusion | flops 429457408 | bytes 15880208 | tf_op jit(solution)/shard_map/bsd,bdr->bsr/dot_general | solution.py:63
  466.7 48.0 %fusion.17 = f32[16,128,3072]{2,1,0:T(8,128)} fusion(bf16[3072,3072]{1,0:T(8,128)(2,1)} %param.42, bf16[16,128,3072]{2,1,0:T(8,128)(2,1)} %all-gather.14.cloned.1.call-done, f32[3072]{0:T(1024)S(1)} %copy-done.21, f32[16,128]{1,0:T(8,128)S(1)} %add_rsqrt_fusion), kind=kOutput, calls=%fused_computation.37 | convolution fusion | flops 38679871488 | bytes 56643584 | tf_op jit(solution)/shard_map/bsd,df->bsf/dot_general | solution.py:65
  514.7 19.3 %fusion.8 = f32[16,128,3072]{2,1,0:T(8,128)} fusion(bf16[16,128,256]{1,2,0:T(8,128)(2,1)} %all-gather.16.cloned.1.call-done, bf16[16,256,3072]{2,1,0:T(8,128)(2,1)} %gather_fusion.10, pred[16]{0:T(512)(128)(4,1)S(1)} %compare_and_fusion), kind=kOutput, calls=%fused_computation.27 | convolution fusion | flops 3233808384 | bytes 51380240 | tf_op jit(solution)/shard_map/bsr,brf->bsf/dot_general | solution.py:66
  534.0 19.3 %fusion.6 = f32[16,128,3072]{2,1,0:T(8,128)} fusion(bf16[16,128,256]{1,2,0:T(8,128)(2,1)} %all-gather.18.cloned.1.call-done, bf16[16,256,3072]{2,1,0:T(8,128)(2,1)} %gather_fusion.12, pred[16]{0:T(512)(128)(4,1)S(1)} %compare_and_fusion), kind=kOutput, calls=%fused_computation.25 | convolution fusion | flops 3233808384 | bytes 51380240 | tf_op jit(solution)/shard_map/bsr,brf->bsf/dot_general | solution.py:66
  553.2 57.7 %multiply_convert_fusion = bf16[16,128,3072]{2,1,0:T(8,128)(2,1)} fusion(f32[16,128,3072]{2,1,0:T(8,128)} %fusion.17, f32[16,128,3072]{2,1,0:T(8,128)} %fusion.6, f32[16,128,3072]{2,1,0:T(8,128)} %fusion.8, bf16[3072,3072]{1,0:T(8,128)(2,1)} %param.41, bf16[16,128,3072]{2,1,0:T(8,128)(2,1)} %all-gather.14.cloned.1.call-done, f32[3072]{0:T(1024)S(1)} %copy-done.21, ...), kind=kOutput, calls=%fused_computation.31 | convolution fusion | flops 38742786048 | bytes 119558144 | tf_op jit(solution)/shard_map/bsd,df->bsf/dot_general | solution.py:65
  610.9 47.0 %fusion.32 = bf16[16,128,3072]{2,1,0:T(8,128)(2,1)} fusion(bf16[16,128,3072]{2,1,0:T(8,128)(2,1)} %multiply_convert_fusion, bf16[3072,3072]{1,0:T(8,128)(2,1)} %param.43), kind=kOutput, calls=%fused_computation.55 | convolution fusion | flops 38660997120 | bytes 44040192 | tf_op jit(solution)/shard_map/bsf,fd->bsd/dot_general | solution.py:69
  657.9 16.7 %copy.54 = bf16[16,128,3072]{1,0,2:T(8,128)(2,1)} copy(bf16[16,128,3072]{2,1,0:T(8,128)(2,1)} %fusion.32) | data formatting | bytes 25165824
  674.6 13.4 %copy.91 = bf16[384,8,16,128]{3,1,2,0:T(8,128)(2,1)} copy(bf16[384,8,16,128]{3,2,1,0:T(8,128)(2,1)} %bitcast.104) | data formatting | bytes 25165824
  688.1 14.7 %gather_fusion.1 = bf16[16,3072,256]{2,1,0:T(8,128)(2,1)} fusion(bf16[8,3072,256]{2,1,0:T(8,128)(2,1)} %param.56, s32[1024]{0:T(1024)} %copy-done.17), kind=kCustom, calls=%fused_computation.13 | custom fusion | bytes 50331712 | tf_op jit(solution)/shard_map/jit(_take)/gather | solution.py:60
  702.9 14.9 %fusion.102 = bf16[16,128,256]{2,1,0:T(8,128)(2,1)} fusion(bf16[16,128,3072]{2,1,0:T(8,128)(2,1)} %multiply_convert_fusion, bf16[16,3072,256]{2,1,0:T(8,128)(2,1)} %gather_fusion.1, pred[16]{0:T(512)(128)(4,1)S(1)} %copy-done.16), kind=kOutput, calls=%fused_computation.125 | convolution fusion | flops 3234332672 | bytes 38797328 | tf_op jit(solution)/shard_map/bsf,bfr->bsr/dot_general | solution.py:70
  720.7 36.6 %reduce-scatter.9.cloned.1.call-done = bf16[384,2048]{1,0:T(8,128)(2,1)} async-done(((bf16[3072,2048]{1,0:T(8,128)(2,1)}), bf16[384,2048]{1,0:T(8,128)(2,1)}) %reduce-scatter.9.cloned.1.call-update) | async-done | bytes 1572880
  761.2 52.7 %all-reduce.5.cloned.1.call-done = bf16[16,128,256]{2,1,0:T(8,128)(2,1)} async-done(((bf16[16,128,256]{2,1,0:T(8,128)(2,1)}), bf16[16,128,256]{2,1,0:T(8,128)(2,1)}) %all-reduce.5.cloned.1.call-update) | async-done | bytes 1048592 | tf_op jit(solution)/shard_map/psum | solution.py:71
  819.0 65.9 %all-gather.20.cloned.1.call-done = bf16[16,128,3072]{2,1,0:T(8,128)(2,1)} async-done(((bf16[16,128,384]{2,1,0:T(8,128)(2,1)}), bf16[16,128,3072]{2,1,0:T(8,128)(2,1)}) %all-gather.20.cloned.1.call-update) | async-done | bytes 12582928 | tf_op jit(solution)/shard_map/all_gather | solution.py:75
  884.9 10.8 %copy.96 = bf16[16,128,3072]{2,1,0:T(8,128)(2,1)} copy(bf16[16,128,3072]{2,1,0:T(8,128)(2,1)} %all-gather.20.cloned.1.call-done) | data formatting | bytes 25165824
  (104 shorter events, 99.9 us)
Async XLA Ops:
  6.5 158.7 %copy-start = (bf16[2,256,3072]{2,1,0:T(8,128)(2,1)S(1)}, bf16[2,256,3072]{2,1,0:T(8,128)(2,1)}, u32[]{:S(2)}) copy-start(bf16[2,256,3072]{2,1,0:T(8,128)(2,1)} %param.40) | copy-start | bytes 9437188
  6.6 135.6 %all-gather.12.cloned.1.call-start = ((), (), s32[]{:S(2)}) async-start(), calls=%async_computation.4 | async-start | bytes 1179648 | tf_op jit(solution)/shard_map/all_gather | solution.py:64
  8.2 525.8 %copy-start.15 = (pred[16]{0:T(512)(128)(4,1)}, pred[16]{0:T(512)(128)(4,1)S(1)}, u32[]{:S(2)}) copy-start(pred[16]{0:T(512)(128)(4,1)S(1)} %compare_and_fusion) | copy-start | bytes 52
  8.2 433.7 %copy-start.17 = (s32[1024]{0:T(1024)}, s32[1024]{0:T(1024)S(1)}, u32[]{:S(2)}) copy-start(s32[1024]{0:T(1024)S(1)} %pad_clamp_fusion) | copy-start | bytes 12292
  15.3 3.8 copy-start.20
  29.9 119.0 %all-gather.10.cloned.1.call-start = ((), (), s32[]{:S(2)}) async-start(), calls=%async_computation.3 | async-start | bytes 1179648 | tf_op jit(solution)/shard_map/all_gather | solution.py:64
  44.5 113.1 %all-gather.8.cloned.1.call-start = ((), (), s32[]{:S(2)}) async-start(), calls=%async_computation.2 | async-start | bytes 1179648 | tf_op jit(solution)/shard_map/all_gather | solution.py:64
  59.6 220.0 %reduce-scatter.7.cloned.1.call-start = ((), (), s32[]{:S(2)}) async-start(), calls=%async_computation.11 | async-start | bytes 14155776
  94.3 12.1 %copy-start.18 = (bf16[3072,2,256]{2,1,0:T(2,128)(2,1)S(1)}, bf16[3072,2,256]{2,1,0:T(2,128)(2,1)}, u32[]{:S(2)}) copy-start(bf16[3072,2,256]{2,1,0:T(2,128)(2,1)} %param.38) | copy-start | bytes 9437188
  106.4 11.7 %copy-start.19 = (bf16[3072,2,256]{2,1,0:T(2,128)(2,1)S(1)}, bf16[3072,2,256]{2,1,0:T(2,128)(2,1)}, u32[]{:S(2)}) copy-start(bf16[3072,2,256]{2,1,0:T(2,128)(2,1)} %param.39) | copy-start | bytes 9437188
  118.1 11.3 %copy-start.7 = (bf16[16,256,2,256]{3,2,1,0:T(2,128)(2,1)S(1)}, bf16[16,256,2,256]{3,2,1,0:T(2,128)(2,1)}, u32[]{:S(2)}) copy-start(bf16[16,256,2,256]{3,2,1,0:T(2,128)(2,1)} %gather_fusion.3) | copy-start | bytes 12582916
  118.1 11.3 %copy-start.8 = (bf16[16,256,2,256]{3,2,1,0:T(2,128)(2,1)S(1)}, bf16[16,256,2,256]{3,2,1,0:T(2,128)(2,1)}, u32[]{:S(2)}) copy-start(bf16[16,256,2,256]{3,2,1,0:T(2,128)(2,1)} %gather_fusion.5) | copy-start | bytes 12582916
  118.2 11.2 %copy-start.9 = (bf16[16,256,2,256]{3,2,1,0:T(2,128)(2,1)S(1)}, bf16[16,256,2,256]{3,2,1,0:T(2,128)(2,1)}, u32[]{:S(2)}) copy-start(bf16[16,256,2,256]{3,2,1,0:T(2,128)(2,1)} %gather_fusion.7) | copy-start | bytes 12582916
  148.8 5.0 copy-start.6
  206.3 1.6 copy-start.10
  206.4 129.8 %all-reduce.3.cloned.1.call-start = ((), (), s32[]{:S(2)}) async-start(), calls=%async_computation.5 | async-start | bytes 2097152 | tf_op jit(solution)/shard_map/psum | solution.py:71
  210.7 5.0 copy-start.11
  215.7 191.5 %all-gather.14.cloned.1.call-start = ((), (), s32[]{:S(2)}) async-start(), calls=%async_computation.6 | async-start | bytes 14155776 | tf_op jit(solution)/shard_map/all_gather | solution.py:75
  282.7 58.7 %copy-start.2 = (bf16[8,3072,32]{1,2,0:T(8,128)(2,1)S(1)}, bf16[8,3072,32]{1,2,0:T(8,128)(2,1)}, u32[]{:S(2)}) copy-start(bf16[8,3072,32]{1,2,0:T(8,128)(2,1)} %param.52) | copy-start | bytes 4718596
  341.3 173.4 %all-gather.16.cloned.1.call-start = ((), (), s32[]{:S(2)}) async-start(), calls=%async_computation.7 | async-start | bytes 1179648 | tf_op jit(solution)/shard_map/all_gather | solution.py:64
  343.8 70.5 %copy-start.4 = (bf16[16,3072,32]{1,2,0:T(8,128)(2,1)S(1)}, bf16[16,3072,32]{1,2,0:T(8,128)(2,1)}, u32[]{:S(2)}) copy-start(bf16[16,3072,32]{1,2,0:T(8,128)(2,1)} %gather_fusion.9) | copy-start | bytes 9437188
  343.8 70.5 %copy-start.21 = (f32[3072]{0:T(1024)S(1)}, f32[3072]{0:T(1024)}, u32[]{:S(2)}) copy-start(f32[3072]{0:T(1024)} %param.36) | copy-start | bytes 36868
  424.1 109.8 %all-gather.18.cloned.1.call-start = ((), (), s32[]{:S(2)}) async-start(), calls=%async_computation.8 | async-start | bytes 1179648 | tf_op jit(solution)/shard_map/all_gather | solution.py:64
  424.7 14.8 %copy-start.3 = (bf16[8,3072,32]{1,2,0:T(8,128)(2,1)S(1)}, bf16[8,3072,32]{1,2,0:T(8,128)(2,1)}, u32[]{:S(2)}) copy-start(bf16[8,3072,32]{1,2,0:T(8,128)(2,1)} %param.54) | copy-start | bytes 4718596
  441.9 14.7 %copy-start.5 = (bf16[16,3072,32]{1,2,0:T(8,128)(2,1)S(1)}, bf16[16,3072,32]{1,2,0:T(8,128)(2,1)}, u32[]{:S(2)}) copy-start(bf16[16,3072,32]{1,2,0:T(8,128)(2,1)} %gather_fusion.11) | copy-start | bytes 9437188
  466.4 290.9 %reduce-scatter.9.cloned.1.call-start = ((), (), s32[]{:S(2)}) async-start(), calls=%async_computation.12 | async-start | bytes 14155776
  688.0 14.8 %copy-start.16 = (pred[16]{0:T(512)(128)(4,1)S(1)}, pred[16]{0:T(512)(128)(4,1)}, u32[]{:S(2)}) copy-start(pred[16]{0:T(512)(128)(4,1)} %copy-done.15) | copy-start | bytes 52
  688.0 125.9 %all-reduce.5.cloned.1.call-start = ((), (), s32[]{:S(2)}) async-start(), calls=%async_computation.9 | async-start | bytes 2097152 | tf_op jit(solution)/shard_map/psum | solution.py:71
  702.9 15.1 %copy-start.12 = (bf16[8,256,384]{2,1,0:T(8,128)(2,1)S(1)}, bf16[8,256,384]{2,1,0:T(8,128)(2,1)}, u32[]{:S(2)}) copy-start(bf16[8,256,384]{2,1,0:T(8,128)(2,1)} %param.57) | copy-start | bytes 4718596
  717.9 167.1 %all-gather.20.cloned.1.call-start = ((), (), s32[]{:S(2)}) async-start(), calls=%async_computation.10 | async-start | bytes 14155776 | tf_op jit(solution)/shard_map/all_gather | solution.py:75
  720.7 93.2 %copy-start.14 = (bf16[16,128,384]{2,1,0:T(8,128)(2,1)S(1)}, bf16[16,128,384]{2,1,0:T(8,128)(2,1)}, u32[]{:S(2)}) copy-start(bf16[16,128,384]{2,1,0:T(8,128)(2,1)} %add_convert_fusion.2) | copy-start | bytes 4718596
  884.9 10.8 %copy-start.1 = (bf16[2,256,3072]{2,1,0:T(8,128)(2,1)S(1)}, bf16[2,256,3072]{2,1,0:T(8,128)(2,1)}, u32[]{:S(2)}) copy-start(bf16[2,256,3072]{2,1,0:T(8,128)(2,1)} %param.40) | copy-start | bytes 9437188
  (1 other events, 1.4 us)
Sparse Core Ops, SparseCore 0:
  30.0 24.5 all-gather.11
  56.2 19.8 all-gather.9
  77.7 19.8 all-gather.7
  206.5 73.0 reduce-scatter.6
  281.8 54.2 all-reduce.2
  341.4 65.7 all-gather.13
  424.3 20.4 all-gather.15
  466.6 20.6 all-gather.17
  688.2 69.1 reduce-scatter.8
  759.6 54.2 all-reduce.4
  819.1 65.7 all-gather.19
where the time goes:
time: 912 us; the launch traced here: 903 us
  matrix products  338 us (37%)
  waiting for transfers between devices  334 us (37%)
  local copies, waits for them, and re-layouts  184 us (20%)
  other arithmetic  30.5 us (3%)
  between operations  14 us (2%)
    dot_general x5, matrix products, column_proj(): jnp.einsum(base_form, act_in, weight, preferred_element_type=jnp.float32)  140 us
    all_gather x2, waiting for transfers between devices, row_proj(): return (out_shard, lax.all_gather(out_shard, 'tensor', axis=2, tiled=True))  129 us
    psum x2, waiting for transfers between devices, row_proj(): low_rank = lax.psum(low_part, 'tensor')  106 us
    gather x14, local copies, waits for them, and re-layouts, per_sequence(): return jnp.take(table_stack, adapter_ids, axis=0)  103 us
    unnamed x13, waiting for transfers between devices  98.5 us
    unnamed x53, local copies, waits for them, and re-layouts  80.3 us
    dot_general x2, matrix products, row_proj(): jnp.einsum(base_form, act_in, weight, preferred_element_type=jnp.float32)  58.2 us
    dot_general x5, matrix products, column_proj(): jnp.einsum('bsd,bdr->bsr', act_in, per_sequence(a_stack), preferred_eleme...  50.8 us
  transfers between devices with their start and end apart: 11, of which 6 were waited for; matrix products, arithmetic and copies ran while one was open for 32% of the time, Pallas kernels for 0%

commit v1 on v0

v1 whole, which is shorter than its diff:
```python
import functools

import jax
import jax.numpy as jnp
from jax import lax
from jax.experimental import pallas as pl
from jax.experimental.pallas import tpu as pltpu
from jax.sharding import PartitionSpec as P

ALPHA = 16.0
ROPE_BASE = 10000.0
EPSILON = 1e-5
F32 = jnp.float32
BF16 = jnp.bfloat16
MESH = pl.DeviceIdType.MESH
ANY = pl.BlockSpec(memory_space=pl.ANY)
NT = (((1,), (1,)), ((), ()))

SEQS = 4
TILE_N = 256
TILE_D = 512


def dot(a, b, dims=None):
    if dims is None:
        return jnp.dot(a, b, preferred_element_type=F32)
    return lax.dot_general(a, b, dims, preferred_element_type=F32)


def rank_kernel(ids_ref, x_ref, gain_ref, aq_ref, ak_ref, av_ref, h_ref, low_ref):
    x = x_ref[0].astype(F32)
    inv = lax.rsqrt(jnp.mean(x * x, axis=-1, keepdims=True) + EPSILON)
    h = (x * inv * gain_ref[...]).astype(BF16)
    h_ref[...] = h
    a = jnp.concatenate([aq_ref[0], ak_ref[0], av_ref[0]], axis=0)
    low_ref[...] = dot(a, h, NT).astype(BF16)


def rank_products(ids, x, gain, aq, ak, av):
    batch, seq, dim = x.shape
    rank = aq.shape[1]
    a_spec = pl.BlockSpec((1, rank, dim), lambda b, ids: (ids[b], 0, 0))
    return pl.pallas_call(
        rank_kernel,
        grid_spec=pltpu.PrefetchScalarGridSpec(
            num_scalar_prefetch=1,
            grid=(batch,),
            in_specs=[
                pl.BlockSpec((1, seq, dim), lambda b, ids: (b, 0, 0)),
                pl.BlockSpec((1, dim), lambda b, ids: (0, 0)),
                a_spec, a_spec, a_spec,
            ],
            out_specs=[
                pl.BlockSpec((seq, dim), lambda b, ids: (b, 0)),
                pl.BlockSpec((3 * rank, seq), lambda b, ids: (0, b)),
            ],
        ),
        out_shape=[
            jax.ShapeDtypeStruct((batch * seq, dim), BF16),
            jax.ShapeDtypeStruct((3 * rank, batch * seq), BF16),
        ],
        compiler_params=pltpu.CompilerParams(vmem_limit_bytes=40 * 2**20),
        cost_estimate=pl.CostEstimate(flops=2 * batch * seq * dim * 256, bytes_accessed=4 * batch * seq * dim, transcendentals=0),
        name="rank_products",
    )(ids, x, gain, aq, ak, av)


def attention_kernel(scale, ids_ref, h_ref, low_ref, wq_ref, wk_ref, wv_ref, bq_ref, bk_ref, bv_ref, wo_ref, ao_ref,
                     cos_ref, sin_ref, part_ref, lowo_ref, z_ref, lowp_ref, attn_ref):
    c = pl.program_id(0)
    n_dev = low_ref.shape[0]
    rank = low_ref.shape[1] // 3
    tokens = h_ref.shape[0]
    seq = tokens // SEQS
    head = 2 * cos_ref.shape[1]
    heads = wq_ref.shape[1] // head
    half = head // 2
    h = h_ref[...]
    for p, w_ref in enumerate((wq_ref, wk_ref, wv_ref)):
        z_ref[p] = dot(h, w_ref[...])
        cat = jnp.concatenate([low_ref[d, rank * p:rank * (p + 1), :] for d in range(n_dev)], axis=0)
        lowp_ref[p] = jnp.transpose(cat.astype(F32)).astype(BF16)
    rows_i = lax.broadcasted_iota(jnp.int32, (seq, seq), 0)
    cols_i = lax.broadcasted_iota(jnp.int32, (seq, seq), 1)
    causal = rows_i >= cols_i
    cos = cos_ref[...]
    sin = sin_ref[...]

    def one_seq(s, carry):
        rows = pl.ds(pl.multiple_of(s * seq, seq), seq)
        ident = ids_ref[c * SEQS + s]
        zs = []
        for p, b_ref in enumerate((bq_ref, bk_ref, bv_ref)):
            zs.append(z_ref[p, rows, :] + scale * dot(lowp_ref[p, rows, :], b_ref[ident]))
        for hd in range(heads):
            lo = hd * head

            def rope(z):
                a = z[:, lo:lo + half]
                b = z[:, lo + half:lo + head]
                return jnp.concatenate([a * cos - b * sin, b * cos + a * sin], axis=-1).astype(BF16)

            q = rope(zs[0])
            k = rope(zs[1])
            v = zs[2][:, lo:lo + head].astype(BF16)
            sc = dot(q, k, NT) * (head ** -0.5)
            sc = jnp.where(causal, sc, -1e30)
            e = jnp.exp(sc - jnp.max(sc, axis=-1, keepdims=True))
            pr = (e / jnp.sum(e, axis=-1, keepdims=True)).astype(BF16)
            attn_ref[rows, lo:lo + head] = dot(pr, v).astype(BF16)
        lowo_ref[0, rows, :] = dot(attn_ref[rows, :], ao_ref[ident]).astype(BF16)
        return carry

    lax.fori_loop(0, SEQS, one_seq, 0)
    n_chip = part_ref.shape[2]
    bc = part_ref.shape[4]
    for i in range(n_chip):
        val = dot(attn_ref[...], wo_ref[:, 2 * bc * i:2 * bc * (i + 1)]).astype(BF16)
        part_ref[0, 0, i] = val[:, :bc]
        part_ref[0, 1, i] = val[:, bc:]


def attention_stage(ids, h, low, wq, wk, wv, bq, bk, bv, wo, ao, cos, sin, scale):
    total, dim = h.shape
    tokens = cos.shape[0] * SEQS
    chunks = total // tokens
    n_dev = low.shape[0]
    rank = bq.shape[1]
    bc = dim // n_dev
    n_chip = n_dev // 2
    width = wq.shape[1]

    def whole(a):
        nd = a.ndim
        return pl.BlockSpec(a.shape, lambda c, ids: (0,) * nd, pipeline_mode=pl.Buffered(1))

    return pl.pallas_call(
        functools.partial(attention_kernel, scale),
        grid_spec=pltpu.PrefetchScalarGridSpec(
            num_scalar_prefetch=1,
            grid=(chunks,),
            in_specs=[
                pl.BlockSpec((tokens, dim), lambda c, ids: (c, 0)),
                pl.BlockSpec((n_dev, low.shape[1], tokens), lambda c, ids: (0, 0, c)),
                whole(wq), whole(wk), whole(wv), whole(bq), whole(bk), whole(bv), whole(wo), whole(ao), whole(cos), whole(sin),
            ],
            out_specs=[
                pl.BlockSpec((1, 2, n_chip, tokens, bc), lambda c, ids: (c, 0, 0, 0, 0)),
                pl.BlockSpec((1, tokens, rank), lambda c, ids: (c, 0, 0)),
            ],
            scratch_shapes=[
                pltpu.VMEM((3, tokens, width), F32),
                pltpu.VMEM((3, tokens, rank), BF16),
                pltpu.VMEM((tokens, width), BF16),
            ],
        ),
        out_shape=[
            jax.ShapeDtypeStruct((chunks, 2, n_chip, tokens, bc), BF16),
            jax.ShapeDtypeStruct((chunks, tokens, rank), BF16),
        ],
        compiler_params=pltpu.CompilerParams(vmem_limit_bytes=60 * 2**20),
        cost_estimate=pl.CostEstimate(flops=2 * total * dim * width * 4, bytes_accessed=6 * total * dim, transcendentals=0),
        name="attention_stage",
    )(ids, h, low, wq, wk, wv, bq, bk, bv, wo, ao, cos, sin)


def remote(src, dst, ssem, rsem, dev):
    return pltpu.make_async_remote_copy(src_ref=src, dst_ref=dst, send_sem=ssem, recv_sem=rsem,
                                        device_id={"tensor": dev}, device_id_type=MESH)


class Exchange:
    def __init__(self, place, d2d, q, ra, rb, ol, orr, gat, rs_send, rs_recv, ag_send, ag_recv):
        self.k, self.i, self.n, self.left, self.right, self.partner = place
        self.d2d, self.q, self.ra, self.rb, self.ol, self.orr, self.g = d2d, q, ra, rb, ol, orr, gat
        self.ss, self.sr, self.gs, self.gr = rs_send, rs_recv, ag_send, ag_recv
        rows = gat.shape[2]
        self.rows = rows
        self.a = pl.ds(0, rows // 2)
        self.b = pl.ds(rows // 2, rows // 2)

    def chip(self, off):
        return lax.rem(self.i + off + self.n, self.n)

    def rs_copy(self, t, src=None):
        q, a, b = self.q, self.a, self.b
        up, far, down = self.chip(1), self.chip(2), self.chip(-1)
        if t == 0:
            pair = (src if src is not None else self.d2d, self.d2d, self.partner)
        elif t == 1:
            pair = (q.at[far, a], self.ra, self.right)
        elif t == 2:
            pair = (q.at[up, b], self.ol.at[b], self.right)
        elif t == 3:
            pair = (q.at[far, b], self.rb, self.left)
        elif t == 4:
            pair = (q.at[down, a], self.orr.at[a], self.left)
        elif t == 5:
            pair = (q.at[up, a], self.ol.at[a], self.right)
        else:
            pair = (q.at[down, b], self.orr.at[b], self.left)
        return remote(pair[0], pair[1], self.ss.at[t], self.sr.at[t], pair[2])

    def add(self, dst, terms):
        rows = dst.shape[0]
        slab = min(rows, 64)

        def body(s, carry):
            r = pl.ds(pl.multiple_of(s * slab, slab), slab)
            tot = terms[0][r, :].astype(F32)
            for t in terms[1:]:
                tot = tot + t[r, :].astype(F32)
            dst[r, :] = tot.astype(BF16)
            return carry

        lax.fori_loop(0, rows // slab, body, 0)

    def start_rs(self, own):
        self.rs_copy(0).wait_recv()
        for off, sends in ((2, (1, 3)), (1, (2,)), (-1, (4,)), (0, ())):
            j = self.chip(off)
            self.add(self.q.at[j], (own.at[j], self.d2d.at[j]))
            for t in sends:
                self.rs_copy(t).start()

    def relay_rs(self):
        self.rs_copy(1).wait_recv()
        up = self.q.at[self.chip(1), self.a]
        self.rs_copy(3).wait_recv()
        down = self.q.at[self.chip(-1), self.b]
        self.add(up, (up, self.ra))
        self.rs_copy(5).start()
        self.add(down, (down, self.rb))
        self.rs_copy(6).start()

    def wait_rs(self):
        for t in (2, 4, 5, 6):
            self.rs_copy(t).wait_recv()

    def ag_copy(self, t):
        g, k, i = self.g, self.k, self.i
        up, far, down = self.chip(1), self.chip(2), self.chip(-1)
        src, dev = (
            (g.at[k, i], self.right),
            (g.at[k, i], self.left),
            (g.at[k, i], self.partner),
            (g.at[k, down, self.a], self.right),
            (g.at[k, up, self.b], self.left),
            (g.at[k, down], self.partner),
            (g.at[k, up], self.partner),
            (g.at[k, far], self.partner),
        )[t]
        return remote(src, src, self.gs.at[t], self.gr.at[t], dev)

    def ag_wait(self, t):
        g, k, i = self.g, self.k, self.i
        up, far, down = self.chip(1), self.chip(2), self.chip(-1)
        o = 1 - k
        dst = (
            g.at[k, down],
            g.at[k, up],
            g.at[o, i],
            g.at[k, far, self.a],
            g.at[k, far, self.b],
            g.at[o, down],
            g.at[o, up],
            g.at[o, far],
        )[t]
        remote(dst, dst, self.gs.at[t], self.gr.at[t], self.partner).wait_recv()

    def start_ag(self):
        for t in (0, 1, 2):
            self.ag_copy(t).start()

    def relay_ag(self):
        self.ag_wait(0)
        self.ag_copy(3).start()
        self.ag_wait(1)
        self.ag_copy(4).start()
        self.ag_copy(5).start()
        self.ag_copy(6).start()

    def last_ag(self):
        self.ag_wait(3)
        self.ag_wait(4)
        self.ag_copy(7).start()

    def end_ag(self):
        for t in (2, 5, 6, 7):
            self.ag_wait(t)
        for t in range(8):
            self.ag_copy(t).wait_send()

    def end_rs(self):
        for t in range(1, 7):
            self.rs_copy(t).wait_send()


R1_TICKS = (0, 1, 4, 5, 6, 7, 8, 10, 12, 13, 14, 15, 17)
R2_TICKS = (0, 2, 6, 7, 8, 9, 11, 14, 16, 17)


def mlp_kernel(scale, n_dev, ids_ref, part_hbm, lowo_hbm, x_hbm, bo_hbm, bd_hbm, agu_hbm, gain_ref,
               wg_ref, wu_ref, bg_ref, bu_ref, ad_ref, wd_ref, y_hbm,
               h2, lowg, lowu, m_ref, lowd, x1own, xres, bo, bd, agu,
               q1, d1, ra1, rb1, ol1, or1, g1, lq1, ld1, lra1, lrb1, lol1, lor1, lg1, gu,
               part2, q2, d2, ra2, rb2, ol2, or2, g2, lpart2, lq2, ld2, lra2, lrb2, lol2, lor2, lg2,
               load_sem, own_sem, y_sem, s_sem, r_sem):
    w = pl.program_id(0)
    j = pl.program_id(1)
    me = lax.axis_index("tensor")
    n = n_dev // 2
    i = me // 2
    k = lax.rem(me, 2)
    right = lax.rem(me + 2, n_dev)
    left = lax.rem(me + n_dev - 2, n_dev)
    partner = me + 1 - 2 * k
    place = (k, i, n, left, right, partner)
    chunks, _, _, tokens, bc = part_hbm.shape
    seq = tokens // SEQS
    gate_ticks = m_ref.shape[1] // TILE_N
    dim = h2.shape[2]

    def sems(t):
        return s_sem.at[t, 0], r_sem.at[t, 0], s_sem.at[t, 1], r_sem.at[t, 1]

    e1 = Exchange(place, d1, q1, ra1, rb1, ol1, or1, g1, *sems(0))
    f1 = Exchange(place, ld1, lq1, lra1, lrb1, lol1, lor1, lg1, *sems(1))
    e2 = Exchange(place, d2, q2, ra2, rb2, ol2, or2, g2, *sems(2))
    f2 = Exchange(place, ld2, lq2, lra2, lrb2, lol2, lor2, lg2, *sems(3))
    eg = Exchange(place, None, None, None, None, None, None, gu, *sems(4))

    def loads():
        return [pltpu.make_async_copy(src, dst, load_sem.at[t])
                for t, (src, dst) in enumerate(((bo_hbm, bo), (agu_hbm, agu), (bd_hbm, bd)))]

    def rows_of(s):
        return pl.ds(s * seq, seq)

    def low_rows(ref, s):
        rows = ref.shape[2]
        per = seq // rows
        return jnp.concatenate([ref[b // n, b % n] for b in range(s * per, (s + 1) * per)], axis=0)

    @pl.when((w == 0) & (j == 0))
    def _():
        barrier = pltpu.get_barrier_semaphore()
        for dev in (left, right, partner):
            pl.semaphore_signal(barrier, inc=1, device_id={"tensor": dev}, device_id_type=MESH)
        for cp in loads():
            cp.start()
        pl.semaphore_wait(barrier, 3)

    def own_loads():
        return (
            pltpu.make_async_copy(part_hbm.at[w, k], q1, own_sem.at[0]),
            pltpu.make_async_copy(lowo_hbm.at[w, k], lq1, own_sem.at[1]),
            pltpu.make_async_copy(x_hbm.at[pl.ds(w * tokens, tokens), pl.ds(pl.multiple_of(me * bc, bc), bc)], xres, own_sem.at[2]),
        )

    def p1_0():
        f1.rs_copy(0, lowo_hbm.at[w, 1 - k]).start()
        e1.rs_copy(0, part_hbm.at[w, 1 - k]).start()
        for cp in own_loads():
            cp.start()

    def p1_1():
        for cp in own_loads():
            cp.wait()
        f1.start_rs(lq1)
        e1.start_rs(q1)
        f1.rs_copy(0, lowo_hbm.at[w, 1 - k]).wait_send()
        e1.rs_copy(0, part_hbm.at[w, 1 - k]).wait_send()

    def p1_2():
        f1.relay_rs()
        e1.relay_rs()

    def low_sum(f):
        f.wait_rs()
        f.add(f.g.at[f.k, f.i], (f.q.at[f.i], f.ol, f.orr))
        f.start_ag()

    def final_sum(e, f, resid, table, chunk, keep):
        f.end_ag()
        e.wait_rs()
        for s in range(SEQS):
            r = rows_of(s)
            tot = resid[r, :].astype(F32) + (e.q[e.i, r, :].astype(F32) + e.ol[r, :].astype(F32) + e.orr[r, :].astype(F32))
            ident = ids_ref[chunk * SEQS + s]
            tot = tot + scale * dot(low_rows(f.g, s), table[ident])
            val = tot.astype(BF16)
            e.g[e.k, e.i, r, :] = val
            if keep is not None:
                keep[r, :] = val
        e.start_ag()
        e.end_rs()
        f.end_rs()

    def p1_6():
        @pl.when(w == 0)
        def _():
            for cp in loads():
                cp.wait()

        final_sum(e1, f1, xres, bo, w, x1own.at[w])

    def p1_9():
        e1.end_ag()
        slot = lax.rem(w, 2)
        hc = h2.at[slot]
        slab = 32

        def body(t, carry):
            r = pl.ds(pl.multiple_of(t * slab, slab), slab)
            tot = None
            for b in range(n_dev):
                v = g1[b % 2, b // 2, r, :].astype(F32)
                sq = jnp.sum(v * v, axis=-1, keepdims=True)
                tot = sq if tot is None else tot + sq
            inv = lax.rsqrt(tot / dim + EPSILON)
            for b in range(n_dev):
                v = g1[b % 2, b // 2, r, :].astype(F32)
                hc[r, bc * b:bc * (b + 1)] = (v * inv * gain_ref[:, bc * b:bc * (b + 1)]).astype(BF16)
            return carry

        lax.fori_loop(0, tokens // slab, body, 0)
        for s in range(SEQS):
            ident = ids_ref[w * SEQS + s]
            gu[k, i, :, s * seq:(s + 1) * seq] = dot(agu[ident], hc[rows_of(s), :], NT).astype(BF16)
        eg.start_ag()

    def p1_12():
        eg.end_ag()
        slot = lax.rem(w, 2)
        half = gu.shape[2] // 2
        for p, ref in enumerate((lowg, lowu)):
            cat = jnp.concatenate([gu[d % 2, d // 2, half * p:half * (p + 1), :] for d in range(n_dev)], axis=0)
            ref[slot] = jnp.transpose(cat.astype(F32)).astype(BF16)

    steps1 = (p1_0, p1_1, p1_2, lambda: low_sum(f1), f1.relay_ag, f1.last_ag, p1_6, e1.relay_ag, e1.last_ag,
              p1_9, eg.relay_ag, eg.last_ag, p1_12)

    def y_copies():
        rows = pl.ds((w - 2) * tokens, tokens)
        return [pltpu.make_async_copy(g2.at[b % 2, b // 2], y_hbm.at[rows, pl.ds(b * bc, bc)], y_sem.at[b]) for b in range(n_dev)]

    def p2_0():
        f2.rs_copy(0, lpart2.at[1 - k]).start()
        e2.rs_copy(0, part2.at[1 - k]).start()

    def p2_1():
        f2.start_rs(lpart2.at[k])
        e2.start_rs(part2.at[k])
        f2.rs_copy(0, lpart2.at[1 - k]).wait_send()
        e2.rs_copy(0, part2.at[1 - k]).wait_send()

    def p2_2():
        f2.relay_rs()
        e2.relay_rs()

    def p2_6():
        final_sum(e2, f2, x1own.at[w - 2], bd, w - 2, None)

    def p2_9():
        e2.end_ag()
        for cp in y_copies():
            cp.start()
        for cp in y_copies():
            cp.wait()

    steps2 = (p2_0, p2_1, p2_2, lambda: low_sum(f2), f2.relay_ag, f2.last_ag, p2_6, e2.relay_ag, e2.last_ag, p2_9)

    for tick, step in zip(R1_TICKS, steps1):
        pl.when((w < chunks) & (j == tick))(step)
    for tick, step in zip(R2_TICKS, steps2):
        pl.when((w >= 2) & (j == tick))(step)

    live = (w >= 1) & (w <= chunks)

    @pl.when(live & (j == 0))
    def _():
        lowd[...] = jnp.zeros_like(lowd)

    @pl.when(live & (j < gate_ticks))
    def _():
        slot = lax.rem(w + 1, 2)
        g = dot(h2[slot], wg_ref[...])
        u = dot(h2[slot], wu_ref[...])
        cols = pl.ds(pl.multiple_of(j * TILE_N, TILE_N), TILE_N)
        for s in range(SEQS):
            r = rows_of(s)
            ident = ids_ref[(w - 1) * SEQS + s]
            gs = g[s * seq:(s + 1) * seq] + scale * dot(lowg[slot, r, :], bg_ref[ident])
            us = u[s * seq:(s + 1) * seq] + scale * dot(lowu[slot, r, :], bu_ref[ident])
            mm = (jax.nn.silu(gs) * us).astype(BF16)
            m_ref[r, cols] = mm
            lowd[r, :] += dot(mm, ad_ref[ident])

    @pl.when(live & (j == gate_ticks))
    def _():
        rows = lpart2.shape[2]
        for b in range(n_dev):
            lpart2[b // n, b % n] = lowd[b * rows:(b + 1) * rows, :].astype(BF16)

    @pl.when(live & (j >= gate_ticks))
    def _():
        jj = j - gate_ticks
        val = dot(m_ref[...], wd_ref[...]).astype(BF16)
        per = bc // 128
        for t in range(TILE_D // 128):
            unit = jj * (TILE_D // 128) + t
            b = unit // per
            off = pl.multiple_of((unit - b * per) * 128, 128)
            part2[lax.rem(b, 2), b // 2, :, pl.ds(off, 128)] = val[:, t * 128:(t + 1) * 128]


def mlp_stage(ids, part, lowo, x, bo, bd, agu, gain, wg, wu, bg, bu, ad, wd, scale, n_dev):
    chunks, _, n_chip, tokens, bc = part.shape
    total, dim = x.shape
    ffn = wg.shape[1]
    n_ad, rank = bo.shape[0], bo.shape[1]
    lrows = tokens // n_dev
    gur = agu.shape[1]
    gt = ffn // TILE_N
    dt = dim // TILE_D

    def gate_idx(w, j):
        t = jnp.minimum(j, gt - 1)
        return jnp.where(w == 0, 0, jnp.where(w > chunks, gt - 1, t))

    def down_idx(w, j):
        t = jnp.maximum(j - gt, 0)
        return jnp.where(w == 0, 0, jnp.where(w > chunks, dt - 1, t))

    def bufs(rows, cols):
        blk = (n_chip, rows, cols)
        return [
            pltpu.VMEM(blk, BF16), pltpu.VMEM(blk, BF16), pltpu.VMEM((rows // 2, cols), BF16), pltpu.VMEM((rows // 2, cols), BF16),
            pltpu.VMEM((rows, cols), BF16), pltpu.VMEM((rows, cols), BF16), pltpu.VMEM((2,) + blk, BF16),
        ]

    return pl.pallas_call(
        functools.partial(mlp_kernel, scale, n_dev),
        grid=(chunks + 2, gt + dt),
        in_specs=[
            pl.BlockSpec(memory_space=pltpu.SMEM), ANY, ANY, ANY, ANY, ANY, ANY,
            pl.BlockSpec((1, dim), lambda w, j: (0, 0)),
            pl.BlockSpec((dim, TILE_N), lambda w, j: (0, gate_idx(w, j))),
            pl.BlockSpec((dim, TILE_N), lambda w, j: (0, gate_idx(w, j))),
            pl.BlockSpec((n_ad, rank, TILE_N), lambda w, j: (0, 0, gate_idx(w, j))),
            pl.BlockSpec((n_ad, rank, TILE_N), lambda w, j: (0, 0, gate_idx(w, j))),
            pl.BlockSpec((n_ad, TILE_N, rank), lambda w, j: (0, gate_idx(w, j), 0)),
            pl.BlockSpec((ffn, TILE_D), lambda w, j: (0, down_idx(w, j))),
        ],
        out_specs=ANY,
        out_shape=jax.ShapeDtypeStruct((total, dim), BF16),
        scratch_shapes=[
            pltpu.VMEM((2, tokens, dim), BF16),
            pltpu.VMEM((2, tokens, rank), BF16),
            pltpu.VMEM((2, tokens, rank), BF16),
            pltpu.VMEM((tokens, ffn), BF16),
            pltpu.VMEM((tokens, rank), F32),
            pltpu.VMEM((chunks, tokens, bc), BF16),
            pltpu.VMEM((tokens, bc), BF16),
            pltpu.VMEM(bo.shape, BF16),
            pltpu.VMEM(bd.shape, BF16),
            pltpu.VMEM(agu.shape, BF16),
            *bufs(tokens, bc),
            *bufs(lrows, rank),
            pltpu.VMEM((2, n_chip, gur, tokens), BF16),
            pltpu.VMEM((2, n_chip, tokens, bc), BF16),
            *bufs(tokens, bc),
            pltpu.VMEM((2, n_chip, lrows, rank), BF16),
            *bufs(lrows, rank),
            pltpu.SemaphoreType.DMA((3,)),
            pltpu.SemaphoreType.DMA((3,)),
            pltpu.SemaphoreType.DMA((n_dev,)),
            pltpu.SemaphoreType.DMA((5, 2, 8)),
            pltpu.SemaphoreType.DMA((5, 2, 8)),
        ],
        compiler_params=pltpu.CompilerParams(collective_id=0, has_side_effects=True, vmem_limit_bytes=67043328),
        name="mlp_stage",
    )(ids, part, lowo, x, bo, bd, agu, gain, wg, wu, bg, bu, ad, wd)


def solution(mesh):
    tp_size = mesh.shape['tensor']
    head_split = P(None, 'tensor', None)
    last_split = P(None, None, 'tensor')
    b_head_split = P(None, None, 'tensor', None)
    in_specs = (P('data', None, None), P('data'), P(None), P(None),
                head_split, head_split, head_split, P('tensor', None, None),
                P(None, 'tensor'), P(None, 'tensor'), P('tensor', None),
                last_split, b_head_split, last_split, b_head_split, last_split, b_head_split,
                P(None, 'tensor', None, None), last_split,
                last_split, last_split, last_split, last_split,
                P(None, 'tensor', None), last_split)

    def local_layer(x_in, adapter_ids, gain_attn, gain_mlp, w_q, w_k, w_v, w_o, w_gate, w_up, w_down, a_q, b_q, a_k, b_k, a_v, b_v, a_o, b_o, a_gate, b_gate, a_up, b_up, a_down, b_down):
        scale = ALPHA / b_q.shape[1]
        batch, seq, dim = x_in.shape
        head = w_q.shape[2]
        half = head // 2
        n_ad, rank = b_q.shape[:2]

        def flip(a):
            return jnp.swapaxes(a, 1, 2)

        def flat(w):
            return w.reshape(w.shape[:-2] + (w.shape[-2] * w.shape[-1],))

        h, low = rank_products(adapter_ids, x_in, gain_attn[None, :], flip(a_q), flip(a_k), flip(a_v))
        low_all = lax.all_gather(low, 'tensor', axis=0)
        inv_freq = ROPE_BASE ** (-2.0 * jnp.arange(half, dtype=F32) / head)
        angle = jnp.arange(seq, dtype=F32)[:, None] * inv_freq[None, :]
        part, lowo = attention_stage(adapter_ids, h, low_all, flat(w_q), flat(w_k), flat(w_v), flat(b_q), flat(b_k), flat(b_v),
                                     w_o.reshape(-1, dim), a_o.reshape(n_ad, -1, rank), jnp.cos(angle), jnp.sin(angle), scale)
        chunks, tokens = lowo.shape[:2]
        lowo = lowo.reshape(chunks, 2, tp_size // 2, tokens // tp_size, rank)
        agu = jnp.concatenate([flip(a_gate), flip(a_up)], axis=1)
        y = mlp_stage(adapter_ids, part, lowo, x_in.reshape(batch * seq, dim), b_o, b_down, agu, gain_mlp[None, :],
                      w_gate, w_up, b_gate, b_up, a_down, w_down, scale, tp_size)
        return y.reshape(batch, seq, dim)

    return jax.shard_map(local_layer, mesh=mesh, in_specs=in_specs, out_specs=P('data', None, None), check_vma=False)
```

time: 912 us -> 511 us (0.56)
  Pallas kernels: 0 us -> 451 us
  matrix products: 338 us -> 0 us
  waiting for transfers between devices: 334 us -> 6.71 us
  local copies, waits for them, and re-layouts: 184 us -> 33.8 us
  other arithmetic: 30.5 us -> 4.73 us
    pallas_call x0 -> x3, Pallas kernels: none -> 451 us  [the longest x1 382 us: mlp_stage(): pl.pallas_call(functools.partial(mlp_kernel, scale, n_dev), grid=(chunks...]
    dot_general x22 -> x0, matrix products: 338 us -> none  [the longest x5 140 us: column_proj(): jnp.einsum(base_form, act_in, weight, preferred_element_type=jnp.float32)]
    all_gather x7 -> x1, waiting for transfers between devices: 129 us -> 6.65 us  [local_layer(): low_all = lax.all_gather(low, 'tensor', axis=0)]
    psum x2 -> x0, waiting for transfers between devices: 106 us -> none  [row_proj(): low_rank = lax.psum(low_part, 'tensor')]
    gather x14 -> x0, local copies, waits for them, and re-layouts: 103 us -> none  [per_sequence(): return jnp.take(table_stack, adapter_ids, axis=0)]
    unnamed x13 -> x1, waiting for transfers between devices: 98.5 us -> 0.05 us
    unnamed x53 -> x24, local copies, waits for them, and re-layouts: 80.3 us -> 24 us
    reduce_sum x3 -> x0, other arithmetic: 14.7 us -> none  [the longest x2 14.2 us: rms_gain(): jnp.mean(act_f32 * act_f32, axis=-1, keepdims=True) + EPSILON]
  transfers between devices with their start and end apart: 11 -> 1, of which waited for: 6 -> 1; matrix products, arithmetic and copies ran while one was open for 32% -> 4% of each run, Pallas kernels for 0% -> 0%
where the time goes in v1:
time: 511 us; the launch traced here: 510 us
  Pallas kernels  451 us (88%)
  local copies, waits for them, and re-layouts  33.8 us (7%)
  between operations  13.5 us (3%)
  waiting for transfers between devices  6.71 us (1%)
    pallas_call x1, Pallas kernels, mlp_stage(): pl.pallas_call(functools.partial(mlp_kernel, scale, n_dev), grid=(chunks...  382 us
    pallas_call x1, Pallas kernels, attention_stage(): pl.pallas_call(functools.partial(attention_kernel, scale), grid_spec=pltp...  51.4 us
    unnamed x24, local copies, waits for them, and re-layouts  24 us
    pallas_call x1, Pallas kernels, rank_products(): pl.pallas_call(rank_kernel, grid_spec=pltpu.PrefetchScalarGridSpec(num_sc...  17.7 us
  transfers between devices with their start and end apart: 1, of which 1 were waited for; matrix products, arithmetic and copies ran while one was open for 4% of the time, Pallas kernels for 0%

profile of v1, /device:TPU:81, one launch (start us, length us, event | category | flops | bytes accessed | tf_op | source)
XLA Modules:
  0.0 509.9 jit_solution(10241320439334985719)
XLA Ops:
  6.5 0.0 all-gather.3.cloned.1.call-start
  6.6 0.0 copy-start
  6.6 1.4 copy-done
  8.0 0.0 copy-start.1
  8.0 1.4 copy-done.1
  9.4 0.0 copy-start.2
  9.4 1.4 copy-done.2
  10.8 0.0 copy-start.3
  10.8 0.7 copy-done.3
  11.5 0.0 copy-start.4
  11.5 0.7 copy-done.4
  12.1 0.0 copy-start.5
  12.1 17.7 %rank_products.1 = (bf16[2048,3072]{1,0:T(8,128)(2,1)}, bf16[96,2048]{1,0:T(8,128)(2,1)}) custom-call(s32[16]{0:T(128)S(1)} %copy-done.4, bf16[16,128,3072]{2,1,0:T(8,128)(2,1)} %x_ref.1, f32[1,3072]{1,0:T(1,128)S(1)} %bitcast.22, bf16[8,32,3072]{2,1,0:T(8,128)(2,1)S(1)} %bitcast.19, bf16[8,32,3072]{2,1,0:T(8,128)(2,1)S(1)} %bitcast.20, ...), custom_call_target="tpu_custom_call" | custom-call | flops 3221225472 | bytes 25165824 | tf_op jit(solution)/shard_map/rank_products/pallas_call | solution.py:43
  29.9 0.1 all-gather.3.cloned.1.call-update
  29.9 0.0 copy-done.5
  30.0 0.0 copy-start.6
  30.0 2.2 copy.26
  32.2 0.6 copy-done.6
  32.8 2.2 copy.27
  35.0 0.6 copy-done.7
  35.6 2.2 copy.28
  37.8 0.0 copy-done.8
  37.8 2.6 reshape.41.bq_ref
  40.4 4.6 reshape.42.bk_ref
  45.0 0.0 copy-done.9
  45.0 2.6 reshape.43.bv_ref
  47.7 0.9 fusion
  48.6 3.8 pad_maximum_fusion.agu_hbm
  52.4 6.7 %all-gather.3.cloned.1.call-done = bf16[768,2048]{1,0:T(8,128)(2,1)} async-done(((bf16[96,2048]{1,0:T(8,128)(2,1)}), bf16[768,2048]{1,0:T(8,128)(2,1)}) %all-gather.3.cloned.1.call-update) | async-done | bytes 3145744 | tf_op jit(solution)/shard_map/all_gather | solution.py:614
  59.0 51.4 %attention_stage.1 = (bf16[4,2,4,512,384]{4,3,2,1,0:T(8,128)(2,1)}, bf16[4,512,256]{2,1,0:T(8,128)(2,1)}) custom-call(s32[16]{0:T(128)} %ids_ref.5, bf16[2048,3072]{1,0:T(8,128)(2,1)} %get-tuple-element.9.h_ref, bf16[8,96,2048]{2,1,0:T(8,128)(2,1)} %bitcast.36, bf16[3072,512]{1,0:T(8,128)(2,1)} %bitcast.28, bf16[3072,512]{1,0:T(8,128)(2,1)} %bitcast.29, ...), custom_call_target="tpu_custom_call" | custom-call | flops 25769803776 | bytes 37748736 | tf_op jit(solution)/shard_map/attention_stage/pallas_call | solution.py:137
  110.4 382.1 %mlp_stage.1 = bf16[2048,3072]{1,0:T(8,128)(2,1)} custom-call(s32[16]{0:T(128)} %ids_ref.5, bf16[4,2,4,512,384]{4,3,2,1,0:T(8,128)(2,1)} %get-tuple-element.11.part_hbm, bf16[4,2,4,64,256]{4,3,2,1,0:T(8,128)(2,1)} %bitcast.33, bf16[2048,3072]{1,0:T(8,128)(2,1)} %bitcast.24, bf16[8,256,384]{2,1,0:T(8,128)(2,1)} %bo_hbm.1, bf16[8,256,384]{2,1,0:T(8,128)(2,1)} %bd_hbm.1, ...), custom_call_target="tpu_custom_call" | custom-call | tf_op jit(solution)/shard_map/mlp_stage/pallas_call | solution.py:543
  492.5 10.5 %copy.30 = bf16[16,128,3072]{2,1,0:T(8,128)(2,1)} copy(bf16[16,128,3072]{2,1,0:T(8,128)(2,1)} %bitcast.23) | data formatting | bytes 25165824
  (4 shorter events, 0.0 us)
Async XLA Ops:
  6.5 52.5 %all-gather.3.cloned.1.call-start = ((), (), s32[]{:S(2)}) async-start(), calls=%async_computation | async-start | bytes 3538944 | tf_op jit(solution)/shard_map/all_gather | solution.py:614
  6.6 1.4 copy-start
  8.0 1.4 copy-start.1
  9.4 1.4 copy-start.2
  10.8 0.7 copy-start.3
  11.5 0.7 copy-start.4
  12.1 17.8 %copy-start.5 = (bf16[3072,2,256]{2,1,0:T(2,128)(2,1)S(1)}, bf16[3072,2,256]{2,1,0:T(2,128)(2,1)}, u32[]{:S(2)}) copy-start(bf16[3072,2,256]{2,1,0:T(2,128)(2,1)} %param.29) | copy-start | bytes 9437188
  30.0 2.8 copy-start.6
  32.8 2.8 copy-start.7
  35.6 2.2 copy-start.8
  40.4 4.6 copy-start.9
Sparse Core Ops, SparseCore 0:
  30.1 28.9 all-gather.2

commit v2 on v1

v2 whole, which is shorter than its diff:
```python
import functools

import jax
import jax.numpy as jnp
from jax import lax
from jax.experimental import pallas as pl
from jax.experimental.pallas import tpu as pltpu
from jax.sharding import PartitionSpec as P

ALPHA = 16.0
ROPE_BASE = 10000.0
EPSILON = 1e-5
F32 = jnp.float32
BF16 = jnp.bfloat16
MESH = pl.DeviceIdType.MESH
ANY = pl.BlockSpec(memory_space=pl.ANY)
NT = (((1,), (1,)), ((), ()))

SEQS = 4
TILE_N = 256
TILE_D = 512


def dot(a, b, dims=None):
    if dims is None:
        return jnp.dot(a, b, preferred_element_type=F32)
    return lax.dot_general(a, b, dims, preferred_element_type=F32)


def rank_kernel(ids_ref, x_ref, gain_ref, aq_ref, ak_ref, av_ref, h_ref, low_ref):
    x = x_ref[0].astype(F32)
    inv = lax.rsqrt(jnp.mean(x * x, axis=-1, keepdims=True) + EPSILON)
    h = (x * inv * gain_ref[...]).astype(BF16)
    h_ref[...] = h
    a = jnp.concatenate([aq_ref[0], ak_ref[0], av_ref[0]])
    low_ref[...] = jnp.transpose(dot(h, a, NT)).astype(BF16)


def rank_products(ids, x, gain, aq, ak, av):
    batch, seq, dim = x.shape
    rank = aq.shape[1]
    a_spec = pl.BlockSpec((1, rank, dim), lambda b, ids: (ids[b], 0, 0))
    return pl.pallas_call(
        rank_kernel,
        grid_spec=pltpu.PrefetchScalarGridSpec(
            num_scalar_prefetch=1,
            grid=(batch,),
            in_specs=[
                pl.BlockSpec((1, seq, dim), lambda b, ids: (b, 0, 0)),
                pl.BlockSpec((1, dim), lambda b, ids: (0, 0)),
                a_spec, a_spec, a_spec,
            ],
            out_specs=[
                pl.BlockSpec((seq, dim), lambda b, ids: (b, 0)),
                pl.BlockSpec((3 * rank, seq), lambda b, ids: (0, b)),
            ],
        ),
        out_shape=[
            jax.ShapeDtypeStruct((batch * seq, dim), BF16),
            jax.ShapeDtypeStruct((3 * rank, batch * seq), BF16),
        ],
        compiler_params=pltpu.CompilerParams(vmem_limit_bytes=60 * 2**20),
        cost_estimate=pl.CostEstimate(flops=2 * batch * seq * dim * 256, bytes_accessed=4 * batch * seq * dim, transcendentals=0),
        name="rank_products",
    )(ids, x, gain, aq, ak, av)


PIECE = 128


class Remote:
    def __init__(self, src, dst, ssem, rsem, dev):
        self.parts = (src, dst, ssem, rsem, dev)

    def make(self, src, dst):
        _, _, ssem, rsem, dev = self.parts
        return pltpu.make_async_remote_copy(src_ref=src, dst_ref=dst, send_sem=ssem, recv_sem=rsem,
                                            device_id={"tensor": dev}, device_id_type=MESH)

    def pieces(self):
        src, dst = self.parts[:2]
        if len(dst.shape) == 3:
            return [self.make(src.at[p], dst.at[p]) for p in range(dst.shape[0])]
        step = min(PIECE if dst.shape[1] <= 512 else 48, dst.shape[0])
        return [self.make(src.at[pl.ds(p, step)], dst.at[pl.ds(p, step)]) for p in range(0, dst.shape[0], step)]

    def start(self):
        start_all(self)

    def wait_send(self):
        self.make(*self.parts[:2]).wait_send()

    def wait_recv(self):
        self.make(*self.parts[:2]).wait_recv()


def start_all(*copies):
    lists = [c.pieces() for c in copies]
    for t in range(max(len(l) for l in lists)):
        for l in lists:
            if t < len(l):
                l[t].start()


def remote(src, dst, ssem, rsem, dev):
    return Remote(src, dst, ssem, rsem, dev)


def placement(n_dev):
    me = lax.axis_index("tensor")
    k = lax.rem(me, 2)
    return k, me // 2, n_dev // 2, lax.rem(me + n_dev - 2, n_dev), lax.rem(me + 2, n_dev), me + 1 - 2 * k


def greet(place):
    barrier = pltpu.get_barrier_semaphore()
    for dev in place[3:]:
        pl.semaphore_signal(barrier, inc=1, device_id={"tensor": dev}, device_id_type=MESH)
    return barrier


class Exchange:
    def __init__(self, place, d2d, q, ra, rb, ol, orr, gat, rs_send, rs_recv, ag_send, ag_recv):
        self.k, self.i, self.n, self.left, self.right, self.partner = place
        self.d2d, self.q, self.ra, self.rb, self.ol, self.orr, self.g = d2d, q, ra, rb, ol, orr, gat
        self.ss, self.sr, self.gs, self.gr = rs_send, rs_recv, ag_send, ag_recv
        rows = gat.shape[2]
        self.rows = rows
        self.a = pl.ds(0, rows // 2)
        self.b = pl.ds(rows // 2, rows // 2)

    def chip(self, off):
        return lax.rem(self.i + off + self.n, self.n)

    def rs_copy(self, t, src=None):
        q, a, b = self.q, self.a, self.b
        up, far, down = self.chip(1), self.chip(2), self.chip(-1)
        if t == 0:
            pair = (src if src is not None else self.d2d, self.d2d, self.partner)
        elif t == 1:
            pair = (q.at[far, a], self.ra, self.right)
        elif t == 2:
            pair = (q.at[up, b], self.ol.at[b], self.right)
        elif t == 3:
            pair = (q.at[far, b], self.rb, self.left)
        elif t == 4:
            pair = (q.at[down, a], self.orr.at[a], self.left)
        elif t == 5:
            pair = (q.at[up, a], self.ol.at[a], self.right)
        else:
            pair = (q.at[down, b], self.orr.at[b], self.left)
        return remote(pair[0], pair[1], self.ss.at[t], self.sr.at[t], pair[2])

    def add(self, dst, terms):
        rows = dst.shape[0]
        slab = min(rows, 64)

        def body(s, carry):
            r = pl.ds(pl.multiple_of(s * slab, slab), slab)
            tot = terms[0][r, :].astype(F32)
            for t in terms[1:]:
                tot = tot + t[r, :].astype(F32)
            dst[r, :] = tot.astype(BF16)
            return carry

        lax.fori_loop(0, rows // slab, body, 0)

    def start_rs(self, own):
        self.rs_copy(0).wait_recv()
        for off, sends in ((2, (1, 3)), (1, (2,)), (-1, (4,)), (0, ())):
            j = self.chip(off)
            self.add(self.q.at[j], (own.at[j], self.d2d.at[j]))
            if sends:
                start_all(*[self.rs_copy(t) for t in sends])

    def relay_rs(self):
        self.rs_copy(1).wait_recv()
        up = self.q.at[self.chip(1), self.a]
        self.rs_copy(3).wait_recv()
        down = self.q.at[self.chip(-1), self.b]
        self.add(up, (up, self.ra))
        self.rs_copy(5).start()
        self.add(down, (down, self.rb))
        self.rs_copy(6).start()

    def wait_rs(self):
        for t in (2, 4, 5, 6):
            self.rs_copy(t).wait_recv()

    def ag_copy(self, t):
        g, k, i = self.g, self.k, self.i
        up, far, down = self.chip(1), self.chip(2), self.chip(-1)
        a, b = self.a, self.b
        src, dev = (
            (g.at[k, i, a], self.right),
            (g.at[k, i, b], self.left),
            (g.at[k, i], self.partner),
            (g.at[k, down, a], self.right),
            (g.at[k, up, b], self.left),
            (g.at[k, down], self.partner),
            (g.at[k, up], self.partner),
            (g.at[k, far], self.partner),
            (g.at[k, i, b], self.right),
            (g.at[k, i, a], self.left),
        )[t]
        return remote(src, src, self.gs.at[t], self.gr.at[t], dev)

    def ag_wait(self, t):
        g, k, i = self.g, self.k, self.i
        up, far, down = self.chip(1), self.chip(2), self.chip(-1)
        o = 1 - k
        dst = (
            g.at[k, down, self.a],
            g.at[k, up, self.b],
            g.at[o, i],
            g.at[k, far, self.a],
            g.at[k, far, self.b],
            g.at[o, down],
            g.at[o, up],
            g.at[o, far],
            g.at[k, down, self.b],
            g.at[k, up, self.a],
        )[t]
        remote(dst, dst, self.gs.at[t], self.gr.at[t], self.partner).wait_recv()

    def start_ag(self):
        start_all(*[self.ag_copy(t) for t in (0, 1)])
        start_all(*[self.ag_copy(t) for t in (8, 9, 2)])

    def relay_ag(self):
        self.ag_wait(0)
        self.ag_copy(3).start()
        self.ag_wait(1)
        self.ag_copy(4).start()

    def last_ag(self):
        self.ag_wait(8)
        self.ag_copy(5).start()
        self.ag_wait(9)
        self.ag_copy(6).start()
        self.ag_wait(3)
        self.ag_wait(4)
        self.ag_copy(7).start()

    def end_ag(self):
        for t in (2, 5, 6, 7):
            self.ag_wait(t)
        for t in range(10):
            self.ag_copy(t).wait_send()

    def end_rs(self):
        for t in range(1, 7):
            self.rs_copy(t).wait_send()


def gather_only(place, gat, send, recv):
    return Exchange(place, *[None] * 6, gat, None, None, send, recv)


def low_sum(f):
    f.wait_rs()
    f.add(f.g.at[f.k, f.i], (f.q.at[f.i], f.ol, f.orr))
    f.start_ag()


def low_rows(ref, s, seq):
    n, rows = ref.shape[1:3]
    per = seq // rows
    return jnp.concatenate([ref[b // n, b % n] for b in range(s * per, (s + 1) * per)])


def total_block(scale, e, f, resid, table, ids_ref, chunk, keep):
    f.end_ag()
    e.wait_rs()
    seq = e.rows // SEQS
    for s in range(SEQS):
        r = pl.ds(s * seq, seq)
        tot = resid[r, :].astype(F32) + (e.q[e.i, r, :].astype(F32) + e.ol[r, :].astype(F32) + e.orr[r, :].astype(F32))
        tot = tot + scale * dot(low_rows(f.g, s, seq), table[ids_ref[chunk * SEQS + s]])
        val = tot.astype(BF16)
        e.g[e.k, e.i, r, :] = val
        if keep is not None:
            keep[r, :] = val
    e.start_ag()
    e.end_rs()
    f.end_rs()


def exchange_bufs(n_chip, rows, cols):
    blk = (n_chip, rows, cols)
    return [
        pltpu.VMEM(blk, BF16), pltpu.VMEM(blk, BF16), pltpu.VMEM((rows // 2, cols), BF16), pltpu.VMEM((rows // 2, cols), BF16),
        pltpu.VMEM((rows, cols), BF16), pltpu.VMEM((rows, cols), BF16), pltpu.VMEM((2,) + blk, BF16),
    ]


def attention_kernel(scale, n_dev, ids_ref, h_ref, low_hbm, x_hbm, wq_ref, wk_ref, wv_ref, bq_ref, bk_ref, bv_ref, wo_ref, ao_ref,
                     bo_ref, cos_ref, sin_ref, part_ref, lowo_ref, g0_hbm, z_ref, lowp_ref, attn_ref, gat, xres,
                     q1, d1, ra1, rb1, ol1, or1, g1, lq1, ld1, lra1, lrb1, lol1, lor1, lg1, load_sem, s_sem, r_sem):
    step = pl.program_id(0)
    chunks = z_ref.shape[0]
    place = placement(n_dev)
    k, i = place[:2]
    pairs = [ref.at[t] for t in range(4) for ref in (s_sem, r_sem)]
    ex = gather_only(place, gat, s_sem.at[4], r_sem.at[4])
    e1 = Exchange(place, d1, q1, ra1, rb1, ol1, or1, g1, *pairs[:4])
    f1 = Exchange(place, ld1, lq1, lra1, lrb1, lol1, lor1, lg1, *pairs[4:])
    tokens, bc = xres.shape
    load_low = pltpu.make_async_copy(low_hbm, gat.at[k, i], load_sem.at[0])
    cols = pl.ds(pl.multiple_of((2 * i + k) * bc, bc), bc)
    load_x = pltpu.make_async_copy(x_hbm.at[pl.ds(0, tokens), cols], xres, load_sem.at[1])

    @pl.when(step == 0)
    def _():
        barrier = greet(place)
        load_low.start()
        load_x.start()
        load_low.wait()
        load_x.wait()
        pl.semaphore_wait(barrier, 3)
        ex.start_ag()

    first = step == chunks - 1
    pl.when(first)(ex.end_ag)

    @pl.when((step < chunks - 1) | (step == chunks))
    def _():
        h = h_ref[...]
        c = jnp.where(step == chunks, chunks - 1, step)
        for p, w_ref in enumerate((wq_ref, wk_ref, wv_ref)):
            z_ref[c, p] = dot(h, w_ref[...])

    pl.when(step == 1)(ex.relay_ag)
    pl.when(step == 2)(ex.last_ag)

    def p1():
        f1.start_rs(lowo_ref.at[0, k])
        e1.start_rs(part_ref.at[0, k])
        f1.rs_copy(0, lowo_ref.at[0, 1 - k]).wait_send()
        e1.rs_copy(0, part_ref.at[0, 1 - k]).wait_send()

    def relays():
        f1.relay_rs()
        e1.relay_rs()

    def finish():
        e1.last_ag()
        e1.end_ag()
        store = pltpu.make_async_copy(g1, g0_hbm, load_sem.at[2])
        store.start()
        store.wait()

    sums = {
        (chunks + 1, 2): relays,
        (chunks + 2, 0): lambda: low_sum(f1),
        (chunks + 2, 1): f1.relay_ag,
        (chunks + 2, 2): f1.last_ag,
        (chunks + 3, 0): lambda: total_block(scale, e1, f1, xres, bo_ref, ids_ref, 0, None),
        (chunks + 3, 2): e1.relay_ag,
        (chunks + 3, 3): finish,
    }

    def slot(t):
        for (when, where), todo in sums.items():
            if where == t:
                pl.when(step == when)(todo)

    @pl.when(first | (step > chunks))
    def _():
        attend(scale, n_dev, jnp.where(first, 0, step - chunks), slot, ids_ref, (bq_ref, bk_ref, bv_ref), wo_ref, ao_ref, cos_ref, sin_ref,
               part_ref, lowo_ref, z_ref, lowp_ref, attn_ref, gat)

    @pl.when(first)
    def _():
        f1.rs_copy(0, lowo_ref.at[0, 1 - k]).start()
        e1.rs_copy(0, part_ref.at[0, 1 - k]).start()

    pl.when(step == chunks)(p1)


def attend(scale, n_dev, c, slot, ids_ref, b_refs, wo_ref, ao_ref, cos_ref, sin_ref, part_ref, lowo_ref, z_ref, lowp_ref, attn_ref, gat):
    rank = gat.shape[2] // 3
    tokens = z_ref.shape[2]
    seq = tokens // SEQS
    head = 2 * cos_ref.shape[1]
    heads = z_ref.shape[3] // head
    half = head // 2
    toks = pl.ds(pl.multiple_of(c * tokens, tokens), tokens)
    for p in range(3):
        cat = jnp.concatenate([gat[d % 2, d // 2, rank * p:rank * (p + 1), toks] for d in range(n_dev)])
        lowp_ref[p] = jnp.transpose(cat.astype(F32)).astype(BF16)
    rows_i = lax.broadcasted_iota(jnp.int32, (seq, seq), 0)
    cols_i = lax.broadcasted_iota(jnp.int32, (seq, seq), 1)
    causal = rows_i >= cols_i
    cos = cos_ref[...]
    sin = sin_ref[...]

    def one_seq(s, carry):
        rows = pl.ds(pl.multiple_of(s * seq, seq), seq)
        ident = ids_ref[c * SEQS + s]
        zs = []
        for p, b_ref in enumerate(b_refs):
            zs.append(z_ref[c, p, rows, :] + scale * dot(lowp_ref[p, rows, :], b_ref[ident]))
        for hd in range(heads):
            lo = hd * head

            def rope(z):
                a = z[:, lo:lo + half]
                b = z[:, lo + half:lo + head]
                return jnp.concatenate([a * cos - b * sin, b * cos + a * sin], axis=-1).astype(BF16)

            q = rope(zs[0])
            k = rope(zs[1])
            v = zs[2][:, lo:lo + head].astype(BF16)
            sc = dot(q, k, NT) * (head ** -0.5)
            sc = jnp.where(causal, sc, -1e30)
            e = jnp.exp(sc - jnp.max(sc, axis=-1, keepdims=True))
            pr = (e / jnp.sum(e, axis=-1, keepdims=True)).astype(BF16)
            attn_ref[rows, lo:lo + head] = dot(pr, v).astype(BF16)
        low = dot(attn_ref[rows, :], ao_ref[ident]).astype(BF16)
        n, per = lowo_ref.shape[2:4]
        for t in range(seq // per):
            b = s * (seq // per) + t
            lowo_ref[0, b // n, lax.rem(b, n)] = low[t * per:(t + 1) * per]
        return carry

    slot(0)
    lax.fori_loop(0, SEQS // 2, one_seq, 0)
    slot(1)
    lax.fori_loop(SEQS // 2, SEQS, one_seq, 0)
    slot(2)
    n_chip = part_ref.shape[2]
    bc = part_ref.shape[4]
    for i in range(n_chip):
        val = dot(attn_ref[...], wo_ref[:, 2 * bc * i:2 * bc * (i + 1)]).astype(BF16)
        part_ref[0, 0, i] = val[:, :bc]
        part_ref[0, 1, i] = val[:, bc:]
    slot(3)


def attention_stage(ids, h, low, x, wq, wk, wv, bq, bk, bv, wo, ao, bo, cos, sin, scale, n_dev):
    total, dim = h.shape
    tokens = cos.shape[0] * SEQS
    chunks = total // tokens
    rank = bq.shape[1]
    bc = dim // n_dev
    n_chip = n_dev // 2
    width = wq.shape[1]

    def whole(a):
        nd = a.ndim
        return pl.BlockSpec(a.shape, lambda c: (0,) * nd, pipeline_mode=pl.Buffered(1))

    def later(c):
        return jnp.maximum(c - chunks, 0)

    return pl.pallas_call(
        functools.partial(attention_kernel, scale, n_dev),
        grid=(2 * chunks,),
        in_specs=[
            pl.BlockSpec(memory_space=pltpu.SMEM),
            pl.BlockSpec((tokens, dim), lambda c: (jnp.minimum(jnp.where(c < chunks - 1, c, c - 1), chunks - 1), 0)),
            ANY,
            ANY,
            whole(wq), whole(wk), whole(wv), whole(bq), whole(bk), whole(bv), whole(wo), whole(ao), whole(bo), whole(cos), whole(sin),
        ],
        out_specs=[
            pl.BlockSpec((1, 2, n_chip, tokens, bc), lambda c: (later(c),) + (0,) * 4),
            pl.BlockSpec((1, 2, n_chip, tokens // n_dev, rank), lambda c: (later(c),) + (0,) * 4),
            ANY,
        ],
        scratch_shapes=[
            pltpu.VMEM((chunks, 3, tokens, width), F32),
            pltpu.VMEM((3, tokens, rank), BF16),
            pltpu.VMEM((tokens, width), BF16),
            pltpu.VMEM((2, n_chip) + low.shape, BF16),
            pltpu.VMEM((tokens, bc), BF16),
            *exchange_bufs(n_chip, tokens, bc),
            *exchange_bufs(n_chip, tokens // n_dev, rank),
            pltpu.SemaphoreType.DMA((3,)),
            pltpu.SemaphoreType.DMA((5, 10)),
            pltpu.SemaphoreType.DMA((5, 10)),
        ],
        out_shape=[
            jax.ShapeDtypeStruct((chunks, 2, n_chip, tokens, bc), BF16),
            jax.ShapeDtypeStruct((chunks, 2, n_chip, tokens // n_dev, rank), BF16),
            jax.ShapeDtypeStruct((2, n_chip, tokens, bc), BF16),
        ],
        compiler_params=pltpu.CompilerParams(collective_id=1, has_side_effects=True, vmem_limit_bytes=67043328),
        cost_estimate=pl.CostEstimate(flops=2 * total * dim * width * 4, bytes_accessed=6 * total * dim, transcendentals=0),
        name="attention_stage",
    )(ids, h, low, x, wq, wk, wv, bq, bk, bv, wo, ao, bo, cos, sin)


LEAD = 5
TAIL = 10
NEVER = -100
FIRST = (NEVER,) * 9 + (-5, -3, -2, -1)
SECOND = (-5, -1, *range(2, 7), 10, 12, 13, *range(15, 18))
LATER = (7, 11, *range(16, 21), 24, 27, 28, 31, 33, 35)
R1_PLAN = ((0, FIRST), (0, SECOND), (0, LATER), (1, LATER))
DOWN_NEXT = (3, 8, 12, *range(14, 18), 20, 22, 24)
DOWN_THEN = (0, 3, *range(7, 12), 14, 16, 17)
R2_PLAN = ((1, DOWN_NEXT), (2, DOWN_NEXT), (3, DOWN_THEN), (4, tuple(range(TAIL))))


def window_of(tick, per):
    later = jnp.maximum(tick - LEAD, 0)
    return jnp.where(tick < LEAD, 0, 1 + later // per), jnp.where(tick < LEAD, tick, lax.rem(later, per))


def mlp_kernel(scale, n_dev, ids_ref, part_hbm, lowo_hbm, x_hbm, g0_hbm, bo_hbm, bd_hbm, agate_hbm, aup_hbm, gain_ref,
               wg_ref, wu_ref, bg_ref, bu_ref, ad_ref, wd_ref, y_hbm,
               h2, lowg, lowu, m_ref, lowd, x1own, xres, bo, bd, agu,
               q1, d1, ra1, rb1, ol1, or1, g1, lq1, ld1, lra1, lrb1, lol1, lor1, lg1, gu,
               part2, q2, d2, ra2, rb2, ol2, or2, g2, lpart2, lq2, ld2, lra2, lrb2, lol2, lor2, lg2,
               load_sem, own_sem, y_sem, s_sem, r_sem):
    tick = pl.program_id(0)
    me = lax.axis_index("tensor")
    place = placement(n_dev)
    k, i, n = place[:3]
    chunks, _, _, tokens, bc = part_hbm.shape
    seq = tokens // SEQS
    gate_ticks = m_ref.shape[1] // TILE_N
    dim = h2.shape[2]
    per_w = gate_ticks + dim // TILE_D
    w, j = window_of(tick, per_w)

    def sems(t):
        return [ref.at[t, part] for part in range(2) for ref in (s_sem, r_sem)]

    e1 = Exchange(place, d1, q1, ra1, rb1, ol1, or1, g1, *sems(0))
    f1 = Exchange(place, ld1, lq1, lra1, lrb1, lol1, lor1, lg1, *sems(1))
    e2 = Exchange(place, d2, q2, ra2, rb2, ol2, or2, g2, *sems(2))
    f2 = Exchange(place, ld2, lq2, lra2, lrb2, lol2, lor2, lg2, *sems(3))
    eg = gather_only(place, gu, *sems(4)[2:])

    half_gu = agu.shape[1] // 2

    def loads():
        return [pltpu.make_async_copy(src, dst, load_sem.at[t])
                for t, (src, dst) in enumerate(((g0_hbm, g1), (agate_hbm, agu.at[:, :half_gu]), (aup_hbm, agu.at[:, half_gu:]), (g0_hbm.at[k, i], x1own.at[0]), (bo_hbm, bo), (bd_hbm, bd)))]

    def rows_of(s):
        return pl.ds(s * seq, seq)

    @pl.when(tick == 0)
    def _():
        barrier = greet(place)
        for cp in loads():
            cp.start()
        pl.semaphore_wait(barrier, 3)

    def own_loads(c):
        return (
            pltpu.make_async_copy(part_hbm.at[c, k], q1, own_sem.at[0]),
            pltpu.make_async_copy(lowo_hbm.at[c, k], lq1, own_sem.at[1]),
            pltpu.make_async_copy(x_hbm.at[pl.ds(c * tokens, tokens), pl.ds(pl.multiple_of(me * bc, bc), bc)], xres, own_sem.at[2]),
        )

    def p1_0(c):
        f1.rs_copy(0, lowo_hbm.at[c, 1 - k]).start()
        e1.rs_copy(0, part_hbm.at[c, 1 - k]).start()
        for cp in own_loads(c):
            cp.start()

    def p1_1(c):
        for cp in own_loads(c):
            cp.wait()
        f1.start_rs(lq1)
        e1.start_rs(q1)
        f1.rs_copy(0, lowo_hbm.at[c, 1 - k]).wait_send()
        e1.rs_copy(0, part_hbm.at[c, 1 - k]).wait_send()

    def p1_2(c):
        f1.relay_rs()
        e1.relay_rs()

    def final_sum(e, f, resid, table, chunk, keep):
        total_block(scale, e, f, resid, table, ids_ref, chunk, keep)

    def p1_6(c):
        final_sum(e1, f1, xres, bo, c, x1own.at[c])

    def p1_9(c):
        @pl.when(c == 0)
        def _():
            for cp in loads():
                cp.wait()

        pl.when(c > 0)(e1.end_ag)
        hc = h2.at[lax.rem(c, 2)]
        slab = 32

        def body(t, carry):
            r = pl.ds(pl.multiple_of(t * slab, slab), slab)
            tot = None
            for b in range(n_dev):
                v = g1[b % 2, b // 2, r, :].astype(F32)
                tot = v * v if tot is None else tot + v * v
            inv = lax.rsqrt(jnp.sum(tot, axis=-1, keepdims=True) / dim + EPSILON)
            for b in range(n_dev):
                v = g1[b % 2, b // 2, r, :].astype(F32)
                hc[r, bc * b:bc * (b + 1)] = (v * inv * gain_ref[:, bc * b:bc * (b + 1)]).astype(BF16)
            return carry

        lax.fori_loop(0, tokens // slab, body, 0)
        for s in range(SEQS):
            ident = ids_ref[c * SEQS + s]
            low = dot(hc[rows_of(s), :], agu[ident], NT)
            gu[k, i, :, s * seq:(s + 1) * seq] = jnp.transpose(low).astype(BF16)
        eg.start_ag()

    def p1_12(c):
        eg.end_ag()
        slot = lax.rem(c, 2)
        half = gu.shape[2] // 2
        for p, ref in enumerate((lowg, lowu)):
            cat = jnp.concatenate([gu[d % 2, d // 2, half * p:half * (p + 1), :] for d in range(n_dev)])
            ref[slot] = jnp.transpose(cat.astype(F32)).astype(BF16)

    steps1 = (p1_0, p1_1, p1_2, lambda c: low_sum(f1), lambda c: f1.relay_ag(), lambda c: f1.last_ag(), p1_6,
              lambda c: e1.relay_ag(), lambda c: e1.last_ag(), p1_9, lambda c: eg.relay_ag(), lambda c: eg.last_ag(), p1_12)

    def y_copies(c):
        rows = pl.ds(c * tokens, tokens)
        return [pltpu.make_async_copy(g2.at[b % 2, b // 2], y_hbm.at[rows, pl.ds(b * bc, bc)], y_sem.at[b]) for b in range(n_dev)]

    def p2_0(c):
        f2.rs_copy(0, lpart2.at[1 - k]).start()
        e2.rs_copy(0, part2.at[1 - k]).start()

    def p2_1(c):
        f2.start_rs(lpart2.at[k])
        e2.start_rs(part2.at[k])
        f2.rs_copy(0, lpart2.at[1 - k]).wait_send()
        e2.rs_copy(0, part2.at[1 - k]).wait_send()

    def p2_2(c):
        f2.relay_rs()
        e2.relay_rs()

    def p2_6(c):
        final_sum(e2, f2, x1own.at[c], bd, c, None)

    def p2_9(c):
        e2.end_ag()
        for cp in y_copies(c):
            cp.start()
        for cp in y_copies(c):
            cp.wait()

    steps2 = (p2_0, p2_1, p2_2, lambda c: low_sum(f2), lambda c: f2.relay_ag(), lambda c: f2.last_ag(), p2_6,
              lambda c: e2.relay_ag(), lambda c: e2.last_ag(), p2_9)

    def place_steps(plan, steps):
        for t, step in enumerate(steps):
            marks = [LEAD + start * per_w + ticks[t] for start, ticks in plan]
            hit = functools.reduce(jnp.logical_or, [tick == mark for mark in marks])

            def run(step=step, marks=marks):
                chunk = 0
                for mark in marks[1:]:
                    chunk = chunk + jnp.where(tick >= mark, 1, 0)
                step(chunk)

            pl.when(hit)(run)

    place_steps(R1_PLAN, steps1)
    place_steps(R2_PLAN, steps2)

    live = (w >= 1) & (w <= chunks)

    @pl.when(live & (j == 0))
    def _():
        lowd[...] = jnp.zeros_like(lowd)

    @pl.when(live & (j < gate_ticks))
    def _():
        slot = lax.rem(w + 1, 2)
        g = dot(h2[slot], wg_ref[...])
        u = dot(h2[slot], wu_ref[...])
        cols = pl.ds(pl.multiple_of(j * TILE_N, TILE_N), TILE_N)
        for s in range(SEQS):
            r = rows_of(s)
            ident = ids_ref[(w - 1) * SEQS + s]
            gs = g[s * seq:(s + 1) * seq] + scale * dot(lowg[slot, r, :], bg_ref[ident])
            us = u[s * seq:(s + 1) * seq] + scale * dot(lowu[slot, r, :], bu_ref[ident])
            mm = (jax.nn.silu(gs) * us).astype(BF16)
            m_ref[r, cols] = mm
            lowd[r, :] += dot(mm, ad_ref[ident])

    @pl.when(live & (j == gate_ticks))
    def _():
        rows = lpart2.shape[2]
        for b in range(n_dev):
            lpart2[b // n, b % n] = lowd[b * rows:(b + 1) * rows, :].astype(BF16)

    @pl.when(live & (j >= gate_ticks))
    def _():
        jj = j - gate_ticks
        val = dot(m_ref[...], wd_ref[...]).astype(BF16)
        per = bc // 128
        for t in range(TILE_D // 128):
            unit = jj * (TILE_D // 128) + t
            b = unit // per
            off = pl.multiple_of((unit - b * per) * 128, 128)
            part2[lax.rem(b, 2), b // 2, :, pl.ds(off, 128)] = val[:, t * 128:(t + 1) * 128]


def mlp_stage(ids, part, lowo, x, g0, bo, bd, agate, aup, gain, wg, wu, bg, bu, ad, wd, scale, n_dev):
    chunks, _, n_chip, tokens, bc = part.shape
    total, dim = x.shape
    ffn = wg.shape[1]
    n_ad, rank = bo.shape[0], bo.shape[1]
    lrows = tokens // n_dev
    gur = 2 * agate.shape[1]
    gt = ffn // TILE_N
    dt = dim // TILE_D

    def gate_idx(tick):
        w, j = window_of(tick, gt + dt)
        return jnp.where(w == 0, 0, jnp.where(w > chunks, gt - 1, jnp.minimum(j, gt - 1)))

    def down_idx(tick):
        w, j = window_of(tick, gt + dt)
        return jnp.where(w == 0, 0, jnp.where(w > chunks, dt - 1, jnp.maximum(j - gt, 0)))

    bufs = functools.partial(exchange_bufs, n_chip)

    return pl.pallas_call(
        functools.partial(mlp_kernel, scale, n_dev),
        grid=(LEAD + chunks * (gt + dt) + TAIL,),
        in_specs=[
            pl.BlockSpec(memory_space=pltpu.SMEM), ANY, ANY, ANY, ANY, ANY, ANY, ANY, ANY,
            pl.BlockSpec((1, dim), lambda t: (0, 0)),
            pl.BlockSpec((dim, TILE_N), lambda t: (0, gate_idx(t))),
            pl.BlockSpec((dim, TILE_N), lambda t: (0, gate_idx(t))),
            pl.BlockSpec((n_ad, rank, TILE_N), lambda t: (0, 0, gate_idx(t))),
            pl.BlockSpec((n_ad, rank, TILE_N), lambda t: (0, 0, gate_idx(t))),
            pl.BlockSpec((n_ad, TILE_N, rank), lambda t: (0, gate_idx(t), 0)),
            pl.BlockSpec((ffn, TILE_D), lambda t: (0, down_idx(t))),
        ],
        out_specs=ANY,
        out_shape=jax.ShapeDtypeStruct((total, dim), BF16),
        scratch_shapes=[
            pltpu.VMEM((2, tokens, dim), BF16),
            pltpu.VMEM((2, tokens, rank), BF16),
            pltpu.VMEM((2, tokens, rank), BF16),
            pltpu.VMEM((tokens, ffn), BF16),
            pltpu.VMEM((tokens, rank), F32),
            pltpu.VMEM((chunks, tokens, bc), BF16),
            pltpu.VMEM((tokens, bc), BF16),
            pltpu.VMEM(bo.shape, BF16),
            pltpu.VMEM(bd.shape, BF16),
            pltpu.VMEM((n_ad, gur, dim), BF16),
            *bufs(tokens, bc),
            *bufs(lrows, rank),
            pltpu.VMEM((2, n_chip, gur, tokens), BF16),
            pltpu.VMEM((2, n_chip, tokens, bc), BF16),
            *bufs(tokens, bc),
            pltpu.VMEM((2, n_chip, lrows, rank), BF16),
            *bufs(lrows, rank),
            pltpu.SemaphoreType.DMA((6,)),
            pltpu.SemaphoreType.DMA((3,)),
            pltpu.SemaphoreType.DMA((n_dev,)),
            pltpu.SemaphoreType.DMA((5, 2, 10)),
            pltpu.SemaphoreType.DMA((5, 2, 10)),
        ],
        compiler_params=pltpu.CompilerParams(collective_id=0, has_side_effects=True, vmem_limit_bytes=67043328),
        name="mlp_stage",
    )(ids, part, lowo, x, g0, bo, bd, agate, aup, gain, wg, wu, bg, bu, ad, wd)


def solution(mesh):
    tp_size = mesh.shape['tensor']
    free = None
    second = P(free, 'tensor')
    third = P(free, free, 'tensor')
    in_specs = (P('data'), P('data'), P(), P(), *[second] * 3, P('tensor'), second, second, P('tensor'),
                *[third] * 6, second, *[third] * 5, second, third)

    def local_layer(x_in, adapter_ids, gain_attn, gain_mlp, w_q, w_k, w_v, w_o, w_gate, w_up, w_down, a_q, b_q, a_k, b_k, a_v, b_v, a_o, b_o, a_gate, b_gate, a_up, b_up, a_down, b_down):
        scale = ALPHA / b_q.shape[1]
        batch, seq, dim = x_in.shape
        head = w_q.shape[2]
        half = head // 2
        n_ad, rank = b_q.shape[:2]

        def flip(a):
            return jnp.swapaxes(a, 1, 2)

        def flat(w):
            rows = lax.optimization_barrier(w.reshape((-1,) + w.shape[-2:]))
            wide = lax.optimization_barrier(rows.reshape(rows.shape[0], -1))
            return wide.reshape(w.shape[:-2] + wide.shape[1:])

        h, low = rank_products(adapter_ids, x_in, gain_attn[None, :], flip(a_q), flip(a_k), flip(a_v))
        inv_freq = ROPE_BASE ** (-2.0 * jnp.arange(half, dtype=F32) / head)
        angle = jnp.arange(seq, dtype=F32)[:, None] * inv_freq[None, :]
        x = x_in.reshape(batch * seq, dim)
        part, lowo, g0 = attention_stage(adapter_ids, h, low, x, flat(w_q), flat(w_k), flat(w_v), flat(b_q), flat(b_k), flat(b_v),
                                         w_o.reshape(-1, dim), a_o.reshape(n_ad, -1, rank), b_o, jnp.cos(angle), jnp.sin(angle), scale, tp_size)
        y = mlp_stage(adapter_ids, part, lowo, x, g0, b_o, b_down, flip(a_gate), flip(a_up), gain_mlp[None, :],
                      w_gate, w_up, b_gate, b_up, a_down, w_down, scale, tp_size)
        return y.reshape(batch, seq, dim)

    return jax.shard_map(local_layer, mesh=mesh, in_specs=in_specs, out_specs=P('data'), check_vma=False)
```

time: 511 us -> 446 us (0.87)
  Pallas kernels: 451 us -> 418 us
  between operations: 13.5 us -> 0.03 us
  local copies, waits for them, and re-layouts: 33.8 us -> 26.4 us
  waiting for transfers between devices: 6.71 us -> 0 us
    pallas_call x2, Pallas kernels: 434 us -> 400 us  [the longest x1 315 us: mlp_stage(): pl.pallas_call(functools.partial(mlp_kernel, scale, n_dev), grid=(LEAD +...]
    reshape x3 -> x0, local copies, waits for them, and re-layouts: 9.82 us -> none  [flat(): return w.reshape(w.shape[:-2] + (w.shape[-2] * w.shape[-1],))]
    all_gather x1 -> x0, waiting for transfers between devices: 6.65 us -> none  [local_layer(): low_all = lax.all_gather(low, 'tensor', axis=0)]
    unnamed x24 -> x17, local copies, waits for them, and re-layouts: 24 us -> 26.4 us
  transfers between devices with their start and end apart: 1 -> 0, of which waited for: 1 -> 0; matrix products, arithmetic and copies ran while one was open for 4% -> 0% of each run, Pallas kernels for 0% -> 0%
where the time goes in v2:
time: 446 us
  Pallas kernels  418 us (94%)
  local copies, waits for them, and re-layouts  26.4 us (6%)
    pallas_call x1, Pallas kernels, mlp_stage(): pl.pallas_call(functools.partial(mlp_kernel, scale, n_dev), grid=(LEAD +...  315 us
    pallas_call x1, Pallas kernels, attention_stage(): pl.pallas_call(functools.partial(attention_kernel, scale, n_dev), grid=(2...  84.5 us
    unnamed x17, local copies, waits for them, and re-layouts  26.4 us
    pallas_call x1, Pallas kernels, rank_products(): pl.pallas_call(rank_kernel, grid_spec=pltpu.PrefetchScalarGridSpec(num_sc...  18.5 us

profile of v2, /device:TPU:81, one launch (start us, length us, event | category | flops | bytes accessed | tf_op | source)
XLA Modules:
  0.0 445.5 jit_solution(11662631654556477311)
XLA Ops:
  0.0 0.0 copy-start.3
  0.0 0.9 fusion
  0.9 3.4 copy.29
  4.3 0.0 copy-start.4
  4.3 0.0 copy-done.3
  4.3 1.9 copy.30
  6.2 0.0 copy-start
  6.2 0.0 copy-done.4
  6.2 1.8 copy.31
  8.0 0.8 copy-done
  8.9 0.0 copy-start.1
  8.9 2.2 copy.26
  11.0 0.6 copy-done.1
  11.7 0.0 copy-start.2
  11.7 2.2 copy.27
  13.9 0.6 copy-done.2
  14.5 2.2 copy.28
  16.8 18.5 %rank_products.1 = (bf16[2048,3072]{1,0:T(8,128)(2,1)}, bf16[96,2048]{1,0:T(8,128)(2,1)}) custom-call(s32[16]{0:T(128)} %ids_ref.5, bf16[16,128,3072]{2,1,0:T(8,128)(2,1)} %x_ref.1, f32[1,3072]{1,0:T(1,128)} %bitcast.50, bf16[8,32,3072]{2,1,0:T(8,128)(2,1)} %bitcast.46, bf16[8,32,3072]{2,1,0:T(8,128)(2,1)} %bitcast.47, bf16[8,32,3072]{2,1,0:T(8,128)(2,1)} %bitcast.48), custom_call_target="tpu_custom_call" | custom-call | flops 3221225472 | bytes 25165824 | tf_op jit(solution)/shard_map/rank_products/pallas_call | solution.py:43
  35.2 84.5 %attention_stage.1 = (bf16[4,2,4,512,384]{4,3,2,1,0:T(8,128)(2,1)}, bf16[4,2,4,64,256]{4,3,2,1,0:T(8,128)(2,1)}, bf16[2,4,512,384]{3,2,1,0:T(8,128)(2,1)}) custom-call(s32[16]{0:T(128)} %ids_ref.5, bf16[2048,3072]{1,0:T(8,128)(2,1)} %get-tuple-element.10.h_ref, bf16[96,2048]{1,0:T(8,128)(2,1)} %get-tuple-element.11.low_hbm, bf16[2048,3072]{1,0:T(8,128)(2,1)} %bitcast.30, ...), custom_call_target="tpu_custom_call" | custom-call | flops 25769803776 | bytes 37748736 | tf_op jit(solution)/shard_map/attention_stage/pallas_call | solution.py:457
  119.8 315.2 %mlp_stage.1 = bf16[2048,3072]{1,0:T(8,128)(2,1)} custom-call(s32[16]{0:T(128)} %ids_ref.5, bf16[4,2,4,512,384]{4,3,2,1,0:T(8,128)(2,1)} %get-tuple-element.12.part_hbm, bf16[4,2,4,64,256]{4,3,2,1,0:T(8,128)(2,1)} %get-tuple-element.13.lowo_hbm, bf16[2048,3072]{1,0:T(8,128)(2,1)} %bitcast.31, bf16[2,4,512,384]{3,2,1,0:T(8,128)(2,1)} %get-tuple-element.14.g0_hbm, ...), custom_call_target="tpu_custom_call" | custom-call | tf_op jit(solution)/shard_map/mlp_stage/pallas_call | solution.py:731
  435.0 10.5 %copy.33 = bf16[16,128,3072]{2,1,0:T(8,128)(2,1)} copy(bf16[16,128,3072]{2,1,0:T(8,128)(2,1)} %bitcast.29) | data formatting | bytes 25165824
  (1 shorter events, 0.0 us)
Async XLA Ops:
  0.0 4.3 copy-start.3
  4.3 1.9 copy-start.4
  6.2 2.6 copy-start
  8.9 2.8 copy-start.1
  11.7 2.8 copy-start.2
